TPU v7x, 16 devices: a whole 2x2x2 slice. The times are simulated.
16 devices in a mesh: tp: 16 (over z, y, x, core).
Axes of the slice: x: 2, y: 2, z: 2, core: 2. Of those that a mesh axis runs over, the one named last changes fastest.
Arguments:
- x_norm: bfloat16 [1024, 2560], P(None, 'tp')
- hid_act: bfloat16 [1024, 6720], P(None, 'tp')
- dy_in: bfloat16 [2, 1024, 6720], replicated
- dy_out: bfloat16 [1024, 2560], replicated
- w_in: float32 [2, 2560, 6720], P(None, 'tp')
- w_out: float32 [6720, 2560], P('tp')
- row_in: float32 [2, 2560], P(None, 'tp')
- col_in: float32 [2, 6720], replicated
- row_out: float32 [6720], P('tp')
- col_out: float32 [2560], replicated
- beta_two: float32 [], replicated
- rel_step: float32 [], replicated
- clip_rms: float32 [], replicated
- clip_norm: float32 [], replicated
Outputs:
- output 1: float32 [2, 2560, 6720], P(None, 'tp')
- output 2: float32 [2, 2560], P(None, 'tp')
- output 3: float32 [2, 6720], replicated
- output 4: float32 [6720, 2560], P('tp')
- output 5: float32 [6720], P('tp')
- output 6: float32 [2560], replicated
All inputs are finite; a program needn't handle non-finite values.
Results may differ from a plain program's by a relative error of at most 0.001.
Values are sent between devices in bfloat16 or wider.
A program may use at most 1 GiB of HBM per device.

v0:
```python
import jax
import jax.numpy as jnp
from jax import lax
from jax.sharding import PartitionSpec as P

EPS_ONE = 1e-30
EPS_TWO = 1e-3


def local_sums(gradient, weight, row_stat):
    col_sq = jnp.sum(gradient * gradient, axis=-2)
    row_sum = jnp.sum(row_stat, axis=-1, keepdims=True)
    w_sq = jnp.sum(weight * weight, axis=(-2, -1))[..., None]
    return jnp.concatenate([col_sq, row_sum, w_sq], axis=-1)


def apply_update(weight, gradient, row_stat, col_stat, totals, shards, beta_two, rel_step, clip_rms, grad_scale):
    rows_total = gradient.shape[-2] * shards
    col_count = gradient.shape[-1]
    col_sq = totals[..., :-2]
    row_sum = totals[..., -2:-1]
    w_sq = totals[..., -1:]
    mix_new = 1.0 - beta_two
    sq_scale = grad_scale * grad_scale
    scaled = grad_scale * gradient
    sq_grad = scaled * scaled + EPS_ONE
    row_new = beta_two * row_stat + mix_new * jnp.mean(sq_grad, axis=-1)
    col_new = beta_two * col_stat + mix_new * (sq_scale * col_sq / rows_total + EPS_ONE)
    grand_sum = jnp.sum(col_sq, axis=-1, keepdims=True)
    row_level = beta_two * row_sum / rows_total + mix_new * (sq_scale * grand_sum / (rows_total * col_count) + EPS_ONE)
    second = (row_new / row_level)[..., :, None] * col_new[..., None, :]
    update = scaled / jnp.sqrt(second)
    upd_sq = lax.psum(jnp.sum(update * update, axis=(-2, -1)), 'tp')
    upd_rms = jnp.sqrt(upd_sq / (rows_total * col_count))[..., None, None]
    clipped = update / jnp.maximum(1.0, upd_rms / clip_rms)
    w_rms = jnp.sqrt(w_sq / (rows_total * col_count))[..., None]
    step_size = rel_step * jnp.maximum(EPS_TWO, w_rms)
    return (weight - step_size * clipped, row_new, col_new)


def solution(mesh):
    shards = mesh.shape['tp']

    def local_step(x_norm, hid_act, dy_in, dy_out, w_in, w_out, row_in, col_in, row_out, col_out, beta_two, rel_step, clip_rms, clip_norm):
        grad_in = jnp.einsum('ti,ktj->kij', x_norm, dy_in, preferred_element_type=jnp.float32)
        grad_out = jnp.einsum('ti,tj->ij', hid_act, dy_out, preferred_element_type=jnp.float32)
        totals_in = lax.psum(local_sums(grad_in, w_in, row_in), 'tp')
        totals_out = lax.psum(local_sums(grad_out, w_out, row_out), 'tp')
        norm_sq = jnp.sum(totals_in[..., :-2]) + jnp.sum(totals_out[..., :-2])
        grad_scale = jnp.minimum(1.0, clip_norm / jnp.sqrt(norm_sq))
        new_in = apply_update(w_in, grad_in, row_in, col_in, totals_in, shards, beta_two, rel_step, clip_rms, grad_scale)
        new_out = apply_update(w_out, grad_out, row_out, col_out, totals_out, shards, beta_two, rel_step, clip_rms, grad_scale)
        return new_in + new_out

    in_specs = (P(None, 'tp'), P(None, 'tp'), P(), P(), P(None, 'tp', None), P('tp', None),
                P(None, 'tp'), P(), P('tp'), P(), P(), P(), P(), P())
    out_specs = (P(None, 'tp', None), P(None, 'tp'), P(), P('tp', None), P('tp'), P())
    return jax.shard_map(local_step, mesh=mesh, in_specs=in_specs, out_specs=out_specs, check_vma=False)
```

profile of v0, /device:TPU:0, one launch (start us, length us, event | category | flops | bytes accessed | tf_op | source)
XLA Modules:
  0.0 148.4 jit_solution(1039153534812187185)
XLA Ops:
  3.3 1.3 reduce_sum.126
  4.6 3.9 %multiply_reduce_fusion.4 = f32[]{:T(128)} fusion(f32[420,2560]{1,0:T(8,128)} %param.19), kind=kLoop, calls=%fused_computation.12 | loop fusion | flops 2150399 | bytes 4300804 | tf_op jit(solution)/shard_map/reduce_sum | solution.py:13
  8.6 4.7 %multiply_reduce_fusion.1 = f32[2]{0:T(128)S(1)} fusion(f32[2,160,6720]{2,1,0:T(8,128)} %param.18), kind=kLoop, calls=%fused_computation.6 | loop fusion | flops 4300798 | bytes 8601608 | tf_op jit(solution)/shard_map/reduce_sum | solution.py:13
  13.3 0.1 copy.35
  13.4 0.1 reduce_sum.122
  13.5 0.1 copy.34
  13.6 7.0 %multiply_reduce_fusion.5 = (f32[2560]{0:T(1024)S(1)}, f32[420,2560]{1,0:T(8,128)}) fusion(bf16[1024,420]{0,1:T(8,128)(2,1)S(1)} %copy-done, bf16[1024,2560]{1,0:T(8,128)(2,1)} %param.17), kind=kOutput, calls=%fused_computation.13 | convolution fusion | flops 2204157440 | bytes 10414080 | tf_op jit(solution)/shard_map/ti,tj->ij/dot_general | solution.py:46
  20.5 1.4 concatenate.7
  21.9 21.5 %multiply_reduce_fusion.2 = (f32[2,6720]{1,0:T(2,128)S(1)}, f32[2,6720,160]{1,2,0:T(8,128)}) fusion(bf16[2,1024,6720]{1,2,0:T(8,128)(2,1)} %param.16, bf16[1024,160]{0,1:T(8,128)(2,1)S(1)} %copy-done.9), kind=kOutput, calls=%fused_computation.7 | convolution fusion | flops 4408306688 | bytes 36508160 | tf_op jit(solution)/shard_map/ti,ktj->kij/dot_general | solution.py:45
  43.4 0.1 concatenate.6
  43.5 36.1 %all-reduce.1 = (f32[2,6722]{1,0:T(2,128)S(1)}, f32[2562]{0:T(1024)S(1)}) all-reduce(f32[2,6722]{1,0:T(2,128)S(1)} %concatenate.6, f32[2562]{0:T(1024)S(1)} %concatenate.7), channel_id=1, replica_groups=mesh['tp'=16] {'tp'}, use_global_device_ids=true, to_apply=%region_3.0 | all-reduce | flops 16006 | bytes 128048 | tf_op jit(solution)/shard_map/psum | solution.py:47
  79.7 0.6 slice_reduce_fusion.2
  80.3 0.7 slice_reduce_fusion
  83.1 0.2 fusion.9
  83.4 0.6 fusion.11
  86.0 2.9 %add_reduce_fusion = f32[420]{0:T(512)S(1)} fusion(f32[420,2560]{1,0:T(8,128)} %get-tuple-element.35, f32[]{:T(128)S(6)} %min.3), kind=kLoop, calls=%fused_computation.11 | loop fusion | flops 4300380 | bytes 4302484 | tf_op jit(solution)/shard_map/reduce_sum | solution.py:27
  88.9 0.6 broadcast_divide_fusion.1
  89.5 4.1 %multiply_reduce_fusion.3 = f32[]{:T(128)} fusion(f32[420,2560]{1,0:T(8,128)} %get-tuple-element.35, f32[2560]{0:T(1024)S(1)} %multiply_add_fusion.1, f32[420]{0:T(512)S(1)} %get-tuple-element.26, f32[]{:T(128)S(6)} %min.3), kind=kLoop, calls=%fused_computation.9 | loop fusion | flops 5375999 | bytes 4312728 | tf_op jit(solution)/shard_map/reduce_sum | solution.py:33
  93.5 1.2 fusion.1
  94.7 0.6 broadcast_divide_fusion
  95.3 2.6 %multiply_reduce_fusion = f32[2]{0:T(128)S(1)} fusion(f32[2,6720,160]{1,2,0:T(8,128)S(1)} %copy-done.2, f32[2,6720]{1,0:T(2,128)S(1)} %multiply_add_fusion, f32[2,160]{1,0:T(2,128)S(1)} %get-tuple-element.28, f32[]{:T(128)S(6)} %min.3), kind=kLoop, calls=%fused_computation.5 | loop fusion | flops 10751998 | bytes 8656652 | tf_op jit(solution)/shard_map/reduce_sum | solution.py:33
  97.9 32.7 %all-reduce = (f32[2]{0:T(128)S(1)}, f32[]{:T(128)}) all-reduce(f32[2]{0:T(128)S(1)} %multiply_reduce_fusion, f32[]{:T(128)} %multiply_reduce_fusion.3), channel_id=1, replica_groups=mesh['tp'=16] {'tp'}, use_global_device_ids=true, to_apply=%region_13.0 | all-reduce | flops 3 | bytes 24 | tf_op jit(solution)/shard_map/psum | solution.py:33
  131.3 6.8 %multiply_subtract_fusion.1 = f32[420,2560]{1,0:T(8,128)} fusion(f32[420,2560]{1,0:T(8,128)} %param.19, f32[420,2560]{1,0:T(8,128)} %get-tuple-element.35, f32[]{:T(128)S(6)} %max.27, f32[2560]{0:T(1024)S(1)} %multiply_add_fusion.1, f32[420]{0:T(512)S(1)} %get-tuple-element.26, f32[]{:T(128)S(6)} %min.3, f32[]{:T(128)} %bitcast.9), kind=kLoop, calls=%fused_computation.8 | loop fusion | flops 6451200 | bytes 12914332 | tf_op jit(solution)/shard_map/sub | solution.py:38
  138.2 10.2 %multiply_subtract_fusion = f32[2,160,6720]{2,1,0:T(8,128)} fusion(f32[2,160,6720]{2,1,0:T(8,128)} %param.18, f32[2,6720,160]{1,2,0:T(8,128)} %get-tuple-element.33, f32[2]{0:T(128)S(1)} %divide_maximum_fusion, f32[2,6720]{1,0:T(2,128)S(1)} %multiply_add_fusion, f32[2,160]{1,0:T(2,128)S(1)} %get-tuple-element.28, f32[]{:T(128)S(6)} %min.3, ...), kind=kLoop, calls=%fused_computation.4 | loop fusion | flops 12902400 | bytes 25859860 | tf_op jit(solution)/shard_map/sub | solution.py:38
  (25 shorter events, 0.2 us)
Async XLA Ops:
  0.6 12.9 %copy-start = (bf16[1024,420]{0,1:T(8,128)(2,1)S(1)}, bf16[1024,420]{0,1:T(8,128)(2,1)}, u32[]{:S(2)}) copy-start(bf16[1024,420]{0,1:T(8,128)(2,1)} %param.15) | copy-start | bytes 2580484
  0.7 12.7 %copy-start.8 = (f32[2,160]{1,0:T(2,128)S(1)}, f32[2,160]{1,0:T(2,128)}, u32[]{:S(2)}) copy-start(f32[2,160]{1,0:T(2,128)} %param.20) | copy-start | bytes 3844
  13.3 8.7 %copy-start.9 = (bf16[1024,160]{0,1:T(8,128)(2,1)S(1)}, bf16[1024,160]{0,1:T(8,128)(2,1)}, u32[]{:S(2)}) copy-start(bf16[1024,160]{0,1:T(8,128)(2,1)} %param.14) | copy-start | bytes 983044
  21.9 61.4 %copy-start.5 = (f32[2,6720]{1,0:T(2,128)S(1)}, f32[2,6720]{1,0:T(2,128)}, u32[]{:S(2)}) copy-start(f32[2,6720]{1,0:T(2,128)} %param.21) | copy-start | bytes 161284
  21.9 64.0 %copy-start.6 = (f32[2560]{0:T(1024)S(1)}, f32[2560]{0:T(1024)}, u32[]{:S(2)}) copy-start(f32[2560]{0:T(1024)} %param.23) | copy-start | bytes 30724
  21.9 67.0 %copy-start.7 = (f32[420]{0:T(512)S(1)}, f32[420]{0:T(512)}, u32[]{:S(2)}) copy-start(f32[420]{0:T(512)} %param.22) | copy-start | bytes 5044
  83.1 10.4 %copy-start.2 = (f32[2,6720,160]{1,2,0:T(8,128)S(1)}, f32[2,6720,160]{1,2,0:T(8,128)}, u32[]{:S(2)}) copy-start(f32[2,6720,160]{1,2,0:T(8,128)} %get-tuple-element.33) | copy-start | bytes 25804804
  83.4 54.8 %copy-start.3 = (f32[2,6720]{1,0:T(2,128)}, f32[2,6720]{1,0:T(2,128)S(1)}, u32[]{:S(2)}) copy-start(f32[2,6720]{1,0:T(2,128)S(1)} %multiply_add_fusion) | copy-start | bytes 161284
  86.0 45.4 %copy-start.4 = (f32[2560]{0:T(1024)}, f32[2560]{0:T(1024)S(1)}, u32[]{:S(2)}) copy-start(f32[2560]{0:T(1024)S(1)} %multiply_add_fusion.1) | copy-start | bytes 30724
  138.1 10.2 %copy-start.1 = (bf16[1024,420]{0,1:T(8,128)(2,1)S(1)}, bf16[1024,420]{0,1:T(8,128)(2,1)}, u32[]{:S(2)}) copy-start(bf16[1024,420]{0,1:T(8,128)(2,1)} %param.15) | copy-start | bytes 2580484
where the time goes:
time: 149 us; the launch traced here: 148 us
  blocking collectives  68.8 us (46%)
  other arithmetic  40.5 us (27%)
  matrix products  28.5 us (19%)
  between operations  8.14 us (5%)
  local copies, waits for them, and re-layouts  2.39 us (2%)
    psum x1, blocking collectives, local_step(): totals_in = lax.psum(local_sums(grad_in, w_in, row_in), 'tp')  36.1 us
    psum x1, blocking collectives, apply_update(): upd_sq = lax.psum(jnp.sum(update * update, axis=(-2, -1)), 'tp')  32.7 us
    dot_general x1, matrix products, local_step(): jnp.einsum('ti,ktj->kij', x_norm, dy_in, preferred_element_type=jnp.float32)  21.5 us
    sub x2, other arithmetic, apply_update(): return (weight - step_size * clipped, row_new, col_new)  17 us
    reduce_sum x2, other arithmetic, local_sums(): w_sq = jnp.sum(weight * weight, axis=(-2, -1))[..., None]  8.63 us
    dot_general x1, matrix products, local_step(): jnp.einsum('ti,tj->ij', hid_act, dy_out, preferred_element_type=jnp.float32)  6.96 us
    reduce_sum x2, other arithmetic, apply_update(): upd_sq = lax.psum(jnp.sum(update * update, axis=(-2, -1)), 'tp')  6.62 us
    reduce_sum x2, other arithmetic, apply_update(): row_new = beta_two * row_stat + mix_new * jnp.mean(sq_grad, axis=-1)  4.09 us

commit v1 on v0

v1 whole, which is shorter than its diff:
```python
import jax
import jax.numpy as jnp
from jax import lax
from jax.experimental import pallas as pl
from jax.experimental.pallas import tpu as pltpu
from jax.sharding import PartitionSpec as P

EPS_ONE = 1e-30
EPS_TWO = 1e-3
LANES = 128
F32 = jnp.float32
BF16 = jnp.bfloat16

OUT_ROW, IN_ROW, IN_STEP, STAT_ROWS = 0, 32, 64, 160
SCALAR_ROW = 24
GROUPS = ((0, 32), (32, 32), (64, 32), (128, 32), (96, 16), (112, 16))
CHUNK = 512
SUPER = 2048
SLOTS = 2


def lane_to_column(vec, rows):
    n = vec.shape[1]
    r = lax.broadcasted_iota(jnp.int32, (rows, n), 0)
    c = lax.broadcasted_iota(jnp.int32, (rows, n), 1)
    col = jnp.sum(jnp.where(r == c, jnp.broadcast_to(vec, (rows, n)), 0.0), axis=1, keepdims=True)
    full = jnp.broadcast_to(col, (rows, LANES))
    if rows > n:
        full = jnp.where(lax.broadcasted_iota(jnp.int32, (rows, LANES), 0) < n, full, 1.0)
    return full


def column_to_lane(col, n):
    part = col[:, :n]
    r = lax.broadcasted_iota(jnp.int32, part.shape, 0)
    c = lax.broadcasted_iota(jnp.int32, part.shape, 1)
    return jnp.sum(jnp.where(r == c, part, 0.0), axis=0, keepdims=True)


def total(x):
    return jnp.sum(jnp.sum(x, axis=0, keepdims=True), axis=1, keepdims=True)


def stats_kernel(n_dev, x_hbm, h_hbm, dyi_hbm, dyo_hbm, wi_hbm, wo_hbm, ri_hbm, ci_hbm, ro_hbm, co_hbm,
                 beta_s, rel_s, crms_s, cnorm_s,
                 di, do, wi, wo, rcol, acol, cnew, kout,
                 x_v, h_v, ring, tail, dyo_v, ri_v, ci_v, ro_v, co_v,
                 part, pair, recv, cden, bden, rsum, recv2,
                 in_sem, ring_sem, tail_sem, dyo_sem, w_sem,
                 pair_send, pair_recv, all_send, all_recv, two_send, two_recv):
    me = lax.axis_index('tp')
    core = lax.rem(me, 2)
    chip = me // 2
    partner = me + 1 - 2 * core
    nk, ni, nff = di.shape
    no, nd = wo.shape[0], wo.shape[1]
    n_super = nff // SUPER
    tail_cols = nff - n_super * SUPER
    rows_in, rows_out = ni * n_dev, no * n_dev
    no_pad = -(-no // 8) * 8

    barrier = pltpu.get_barrier_semaphore()
    for d in range(1, n_dev):
        pl.semaphore_signal(barrier, inc=1, device_id=(lax.rem(me + d, n_dev),), device_id_type=pl.DeviceIdType.MESH)

    small = [pltpu.make_async_copy(h_hbm, h_v, in_sem.at[0])]
    for a, b in ((ro_hbm, ro_v), (co_hbm, co_v), (ri_hbm, ri_v), (ci_hbm, ci_v), (x_hbm, x_v)):
        small.append(pltpu.make_async_copy(a, b, in_sem.at[len(small)]))
    n_out = nd // CHUNK
    dyo_cp = [pltpu.make_async_copy(dyo_hbm.at[:, pl.ds(c * CHUNK, CHUNK)], dyo_v.at[:, pl.ds(c * CHUNK, CHUNK)],
                                    dyo_sem.at[c]) for c in range(n_out)]
    def super_copy(k, c, slot):
        return pltpu.make_async_copy(dyi_hbm.at[k, pl.ds(c * SUPER, SUPER), :], ring.at[slot], ring_sem.at[slot])

    tail_cp = [pltpu.make_async_copy(dyi_hbm.at[k, pl.ds(n_super * SUPER, tail_cols), :], tail.at[k], tail_sem.at[k])
               for k in range(nk)]
    w_cp = [pltpu.make_async_copy(wi_hbm.at[k], wi.at[k], w_sem.at[k]) for k in range(nk)]
    w_cp.append(pltpu.make_async_copy(wo_hbm, wo, w_sem.at[nk]))

    small[0].start()
    for cp in dyo_cp:
        cp.start()
    for cp in small[1:]:
        cp.start()
    sequence = [(0, 0), (0, 1), (0, 2), (1, 2), (1, 0), (1, 1)]
    super_copy(*sequence[0], 0).start()
    super_copy(*sequence[1], 1).start()
    for cp in tail_cp:
        cp.start()

    part[...] = jnp.zeros_like(part)
    cden[...] = jnp.ones_like(cden)
    for cp in small[1:5]:
        cp.wait()
    for q in range(nd // LANES):
        cden[pl.ds(OUT_ROW + q, 1), :] = co_v[:, pl.ds(q * LANES, LANES)]
    for k in range(nk):
        for q in range(nff // LANES):
            cden[pl.ds(IN_ROW + IN_STEP * k + q, 1), :] = ci_v[pl.ds(k, 1), pl.ds(q * LANES, LANES)]
        rest = nff % LANES
        if rest:
            cden[pl.ds(IN_ROW + IN_STEP * k + nff // LANES, 1), pl.ds(0, rest)] = (
                ci_v[pl.ds(k, 1), pl.ds(nff - rest, rest)])
    for k in range(nk):
        vec = ri_v[pl.ds(k, 1), :]
        for p in range(0, ni, LANES):
            n = min(LANES, ni - p)
            rcol[pl.ds(k * ni + p, n), :] = lane_to_column(vec[:, p:p + n], n)
    vec = ro_v[...]
    for p in range(0, no, LANES):
        n = min(LANES, no - p)
        rows = -(-n // 8) * 8
        rcol[pl.ds(nk * ni + p, rows), :] = lane_to_column(vec[:, p:p + n], rows)
    lane = lax.broadcasted_iota(jnp.int32, (1, LANES), 1)
    row_sums = jnp.where(lane == 0, jnp.sum(ri_v[pl.ds(0, 1), :], axis=1, keepdims=True), 0.0)
    row_sums += jnp.where(lane == 1, jnp.sum(ri_v[pl.ds(1, 1), :], axis=1, keepdims=True), 0.0)
    row_sums += jnp.where(lane == 2, jnp.sum(vec, axis=1, keepdims=True), 0.0)
    part[pl.ds(SCALAR_ROW, 1), :] = row_sums

    def pair_copy(g):
        start, size = GROUPS[g]
        rows = pl.ds(pl.multiple_of(start + (1 - core) * (size // 2), 8), size // 2)
        return pltpu.make_async_remote_copy(src_ref=part.at[rows, :], dst_ref=pair.at[rows, :],
                                            send_sem=pair_send.at[g], recv_sem=pair_recv.at[g],
                                            device_id=(partner,), device_id_type=pl.DeviceIdType.MESH)

    def all_copy(g, d):
        start, size = GROUPS[g]
        rows = pl.ds(pl.multiple_of(start + core * (size // 2), 8), size // 2)
        dest = lax.rem(me + d, n_dev)
        return pltpu.make_async_remote_copy(src_ref=recv.at[chip, rows, :], dst_ref=recv.at[chip, rows, :],
                                            send_sem=all_send.at[g, d], recv_sem=all_recv.at[g, me],
                                            device_id=(dest,), device_id_type=pl.DeviceIdType.MESH)

    def all_wait(g, d):
        start, size = GROUPS[g]
        src = lax.rem(me + d, n_dev)
        rows = pl.ds(pl.multiple_of(start + lax.rem(src, 2) * (size // 2), 8), size // 2)
        ref = recv.at[src // 2, rows, :]
        pltpu.make_async_remote_copy(src_ref=ref, dst_ref=ref, send_sem=all_send.at[g, d], recv_sem=all_recv.at[g, src],
                                     device_id=(src,), device_id_type=pl.DeviceIdType.MESH).wait_recv()

    def spread(g):
        start, size = GROUPS[g]
        pair_copy(g).wait_recv()
        rows = pl.ds(pl.multiple_of(start + core * (size // 2), 8), size // 2)
        recv[chip, rows, :] = part[rows, :] + pair[rows, :]
        for d in range(1, n_dev):
            all_copy(g, d).start()

    rsum[...] = jnp.zeros_like(rsum)

    def square_sums(g, row0, stat0):
        m, n = g.shape
        sq = g * g
        cols = jnp.sum(sq, axis=0, keepdims=True)
        acc = rsum[pl.ds(row0, m), :]
        for b in range(0, n, LANES):
            w = min(LANES, n - b)
            if w == LANES:
                acc += sq[:, b:b + w]
                part[pl.ds(stat0 + b // LANES, 1), :] = cols[:, b:b + w]
            else:
                acc = acc + jnp.concatenate([sq[:, b:b + w], jnp.zeros((m, LANES - w), F32)], axis=1)
                part[pl.ds(stat0 + b // LANES, 1), pl.ds(0, w)] = cols[:, b:b + w]
        rsum[pl.ds(row0, m), :] = acc

    small[0].wait()
    for c in range(n_out):
        dyo_cp[c].wait()
        for p in range(0, CHUNK, 256):
            col = c * CHUNK + p
            g = jnp.dot(h_v[...], dyo_v[:, pl.ds(col, 256)], preferred_element_type=F32)
            do[:, pl.ds(col, 256)] = g
            square_sums(g, nk * ni, OUT_ROW + col // LANES)
    pl.semaphore_wait(barrier, n_dev - 1)
    pair_copy(0).start()

    small[5].wait()

    def nt(dy):
        return lax.dot_general(x_v[...], dy, (((1,), (1,)), ((), ())), preferred_element_type=F32)

    def super_step(k, c, slot):
        for p in range(0, SUPER, 256):
            col = pl.multiple_of(c * SUPER + p, 256)
            g = nt(ring[slot, pl.ds(p, 256), :])
            di[k, :, pl.ds(col, 256)] = g
            square_sums(g, k * ni, IN_ROW + IN_STEP * k + c * (SUPER // LANES) + p // LANES)

    def tail_step(k):
        for p in range(0, tail_cols, 256):
            n = min(256, tail_cols - p)
            col = n_super * SUPER + p
            g = nt(tail[k, pl.ds(p, n), :])
            di[k, :, pl.ds(col, n)] = g
            square_sums(g, k * ni, IN_ROW + IN_STEP * k + col // LANES)

    def step(i):
        slot = i % SLOTS
        super_copy(*sequence[i], slot).wait()
        super_step(*sequence[i], slot)
        if i + SLOTS < len(sequence):
            super_copy(*sequence[i + SLOTS], slot).start()

    step(0)
    step(1)
    pair_copy(1).start()
    spread(0)
    step(2)
    tail_cp[0].wait()
    tail_step(0)
    pair_copy(2).start()
    spread(1)
    step(3)
    tail_cp[1].wait()
    tail_step(1)
    pair_copy(3).start()
    spread(2)
    step(4)
    pair_copy(4).start()
    spread(3)
    for cp in w_cp:
        cp.start()
    step(5)
    pair_copy(5).start()
    spread(4)
    spread(5)

    rsum[...] = jnp.broadcast_to(jnp.sum(rsum[...], axis=1, keepdims=True), rsum.shape)

    def w_square_in(k):
        def body(q, acc):
            w = wi[k, :, pl.ds(pl.multiple_of(q * LANES, LANES), LANES)]
            return acc + w * w
        acc = lax.fori_loop(0, nff // LANES, body, jnp.zeros((ni, LANES), F32))
        rest = nff % LANES
        w = wi[k, :, pl.ds(nff - rest, rest)]
        return total(acc) + total(w * w)

    def w_square_out():
        m = no // 8 * 8
        acc = jnp.zeros((8, nd), F32)
        acc = lax.fori_loop(0, m // 8, lambda i, a: a + jnp.square(wo[pl.ds(pl.multiple_of(i * 8, 8), 8), :]), acc)
        w = wo[pl.ds(m, no - m), :]
        return total(acc) + total(w * w)

    w_sq = []
    for k in range(nk):
        w_cp[k].wait()
        w_sq.append(w_square_in(k))
    w_cp[nk].wait()
    w_sq.append(w_square_out())

    for g in range(len(GROUPS)):
        for d in range(1, n_dev):
            all_wait(g, d)

    beta = jnp.full((1, 1), beta_s[0], F32)
    mix = 1.0 - beta
    tot = recv[0]
    for c in range(1, n_dev // 2):
        tot = tot + recv[c]
    bden[...] = tot
    seg = [(IN_ROW + IN_STEP * k, IN_STEP, k * ni, ni, rows_in, nff) for k in range(nk)]
    seg.append((OUT_ROW, SCALAR_ROW, nk * ni, no_pad, rows_out, nd))
    sums = [total(bden[pl.ds(a, n), :]) for a, n, *_ in seg]
    norm_sq = sums[0] + sums[1] + sums[2]
    scale = jnp.minimum(1.0, jnp.full((1, 1), cnorm_s[0], F32) / jnp.sqrt(norm_sq))
    row_tot = bden[pl.ds(SCALAR_ROW, 1), :]
    for j, (a, n, ra, rn, m_all, n_all) in enumerate(seg):
        c2 = beta * cden[pl.ds(a, n), :] + mix * (scale * (scale * bden[pl.ds(a, n), :]) * (1.0 / m_all) + EPS_ONE)
        cnew[pl.ds(a, n), :] = c2
        bden[pl.ds(a, n), :] = lax.rsqrt(c2)
        r2 = beta * rcol[pl.ds(ra, rn), :] + mix * (scale * (scale * rsum[pl.ds(ra, rn), :]) * (1.0 / n_all) + EPS_ONE)
        rcol[pl.ds(ra, rn), :] = r2
        r_all = jnp.sum(jnp.where(lane == j, row_tot, 0.0), axis=1, keepdims=True)
        level = beta * (r_all / m_all) + mix * (scale * (scale * (sums[j] / n_all)) * (1.0 / m_all) + EPS_ONE)
        acol[pl.ds(ra, rn), :] = lax.rsqrt(r2 / level)

    def u_block(ref, k, row0, m, col, w, brow):
        s = jnp.broadcast_to(scale, (m, w))
        b = jnp.broadcast_to(bden[pl.ds(brow, 1), pl.ds(0, w)], (m, w))
        idx = (pl.ds(row0, m), pl.ds(col, w)) if k is None else (k, pl.ds(row0, m), pl.ds(col, w))
        t = (s * ref[idx]) * b
        ref[idx] = t
        return t * t

    u_sq = []
    for k in range(nk):
        def body(q, acc, k=k):
            return acc + u_block(di, k, 0, ni, pl.multiple_of(q * LANES, LANES), LANES, IN_ROW + IN_STEP * k + q)
        acc = lax.fori_loop(0, nff // LANES, body, jnp.zeros((ni, LANES), F32))
        a = acol[pl.ds(k * ni, ni), :]
        u = total(acc * a * a)
        rest = nff % LANES
        if rest:
            acc = u_block(di, k, 0, ni, nff - rest, rest, IN_ROW + IN_STEP * k + nff // LANES)
            a = acol[pl.ds(k * ni, ni), pl.ds(0, rest)]
            u = u + total(acc * a * a)
        u_sq.append(u)
    u = jnp.zeros((1, 1), F32)
    for row0, m in ((0, 144), (144, 144), (288, no - 288)):
        def body(q, acc, row0=row0, m=m):
            return acc + u_block(do, None, row0, m, pl.multiple_of(q * LANES, LANES), LANES, OUT_ROW + q)
        acc = lax.fori_loop(0, nd // LANES, body, jnp.zeros((m, LANES), F32))
        a = acol[pl.ds(nk * ni + row0, m), :]
        u = u + total(acc * a * a)
    u_sq.append(u)

    msg = jnp.zeros((1, LANES), F32)
    for j in range(3):
        msg = msg + jnp.where(lane == j, u_sq[j], 0.0) + jnp.where(lane == 3 + j, w_sq[j], 0.0)
    recv2[me] = msg

    def two_copy(d):
        dest = lax.rem(me + d, n_dev)
        return pltpu.make_async_remote_copy(src_ref=recv2.at[me], dst_ref=recv2.at[me], send_sem=two_send.at[d],
                                            recv_sem=two_recv.at[me], device_id=(dest,),
                                            device_id_type=pl.DeviceIdType.MESH)

    for d in range(1, n_dev):
        two_copy(d).start()
    for g in range(len(GROUPS)):
        pair_copy(g).wait_send()
        for d in range(1, n_dev):
            all_copy(g, d).wait_send()
    for d in range(1, n_dev):
        src = lax.rem(me + d, n_dev)
        ref = recv2.at[src]
        pltpu.make_async_remote_copy(src_ref=ref, dst_ref=ref, send_sem=two_send.at[d], recv_sem=two_recv.at[src],
                                     device_id=(src,), device_id_type=pl.DeviceIdType.MESH).wait_recv()
    all_sums = recv2[0]
    for c in range(1, n_dev):
        all_sums = all_sums + recv2[c]
    for j, (_, _, _, _, m_all, n_all) in enumerate(seg):
        u = jnp.sum(jnp.where(lane == j, all_sums, 0.0), axis=1, keepdims=True)
        w = jnp.sum(jnp.where(lane == 3 + j, all_sums, 0.0), axis=1, keepdims=True)
        u_rms = jnp.sqrt(u / (m_all * n_all))
        w_rms = jnp.sqrt(w / (m_all * n_all))
        step_size = jnp.full((1, 1), rel_s[0], F32) * jnp.maximum(EPS_TWO, w_rms)
        k = step_size / jnp.maximum(1.0, u_rms / jnp.full((1, 1), crms_s[0], F32))
        kout[pl.ds(j, 1), :] = jnp.broadcast_to(k, (1, LANES))
    for d in range(1, n_dev):
        two_copy(d).wait_send()


B_IN = 32


def update_kernel(di, do, wi, wo, rcol, acol, cnew, kout, wi_out, ri_out, ci_out, wo_out, ro_out, co_out,
                  buf_in, buf_out, sem_in, sem_out):
    nk, ni, nff = di.shape
    nd = do.shape[1]
    no = wo_out.shape[0]
    steps = ni // B_IN

    def in_copy(k, i, slot):
        return pltpu.make_async_copy(buf_in.at[slot], wi_out.at[k, pl.ds(i * B_IN, B_IN), :], sem_in.at[slot])

    def widths(n):
        return [(c, min(LANES, n - c)) for c in range(0, n, LANES)]

    pend = [None] * buf_in.shape[0]
    for k in range(nk):
        kk = jnp.broadcast_to(kout[pl.ds(k, 1), :], (B_IN, LANES))
        for i in range(steps):
            slot = (k * steps + i) % buf_in.shape[0]
            if pend[slot] is not None:
                pend[slot].wait()
            a = acol[pl.ds(k * ni + i * B_IN, B_IN), :]
            rows = pl.ds(i * B_IN, B_IN)

            def body(q, _, k=k, rows=rows, slot=slot, a=a, kk=kk):
                c = pl.ds(pl.multiple_of(q * LANES, LANES), LANES)
                buf_in[slot, :, c] = wi[k, rows, c] - kk * (di[k, rows, c] * a)
                return 0
            lax.fori_loop(0, nff // LANES, body, 0, unroll=4)
            rest = nff % LANES
            if rest:
                c = pl.ds(nff - rest, rest)
                buf_in[slot, :, c] = wi[k, rows, c] - kk[:, :rest] * (di[k, rows, c] * a[:, :rest])
            cp = in_copy(k, i, slot)
            cp.start()
            pend[slot] = cp
    pend_out = [None] * buf_out.shape[0]
    for i in range(nd // CHUNK):
        slot = i % buf_out.shape[0]
        if pend_out[slot] is not None:
            pend_out[slot].wait()
        kk = jnp.broadcast_to(kout[pl.ds(nk, 1), :], (8, LANES))

        def rows_of(o, n, i=i, slot=slot, kk=kk):
            r = pl.ds(o, n)
            a = acol[pl.ds(nk * ni + o, n), :]
            for c in range(0, CHUNK, LANES):
                cc = pl.ds(i * CHUNK + c, LANES)
                buf_out[slot, r, pl.ds(c, LANES)] = wo[r, cc] - kk[:n] * (do[r, cc] * a)

        def body(q, _, rows_of=rows_of):
            rows_of(pl.multiple_of(q * 8, 8), 8)
            return 0
        lax.fori_loop(0, no // 8, body, 0, unroll=4)
        if no % 8:
            rows_of(no // 8 * 8, no % 8)
        cols = pl.ds(i * CHUNK, CHUNK)
        cp = pltpu.make_async_copy(buf_out.at[slot], wo_out.at[:, cols], sem_out.at[slot])
        cp.start()
        pend_out[slot] = cp
    for q in range(nd // LANES):
        co_out[:, pl.ds(q * LANES, LANES)] = cnew[pl.ds(OUT_ROW + q, 1), :]
    for k in range(nk):
        for c, n in widths(nff):
            ci_out[pl.ds(k, 1), pl.ds(c, n)] = cnew[pl.ds(IN_ROW + IN_STEP * k + c // LANES, 1), pl.ds(0, n)]
        for c, n in widths(ni):
            ri_out[pl.ds(k, 1), pl.ds(c, n)] = column_to_lane(rcol[pl.ds(k * ni + c, n), :], n)
    for c, n in widths(no):
        ro_out[:, pl.ds(c, n)] = column_to_lane(rcol[pl.ds(nk * ni + c, -(-n // 8) * 8), :], n)
    for cp in pend + pend_out:
        if cp is not None:
            cp.wait()


def solution(mesh):
    n_dev = mesh.shape['tp']

    def local_step(x_norm, hid_act, dy_in, dy_out, w_in, w_out, row_in, col_in, row_out, col_out,
                   beta_two, rel_step, clip_rms, clip_norm):
        t, ni = x_norm.shape
        no = hid_act.shape[1]
        nk, _, nff = dy_in.shape
        nd = dy_out.shape[1]
        no_pad = -(-no // 8) * 8
        tail_cols = nff - nff // SUPER * SUPER
        vm = pl.BlockSpec(memory_space=pltpu.VMEM)
        hb = pl.BlockSpec(memory_space=pltpu.HBM)
        sm = pl.BlockSpec(memory_space=pltpu.SMEM)
        dma = pltpu.SemaphoreType.DMA
        n_rows = nk * ni + no_pad
        a_out = [pltpu.VMEM((nk, ni, nff), F32), pltpu.VMEM((no, nd), F32),
                 pltpu.VMEM((nk, ni, nff), F32), pltpu.VMEM((no, nd), F32),
                 pltpu.VMEM((n_rows, LANES), F32), pltpu.VMEM((n_rows, LANES), F32),
                 pltpu.VMEM((STAT_ROWS, LANES), F32), pltpu.VMEM((8, LANES), F32)]
        ng = len(GROUPS)
        outs = pl.pallas_call(
            lambda *refs: stats_kernel(n_dev, *refs),
            out_shape=a_out,
            in_specs=[hb] * 10 + [sm] * 4,
            out_specs=[vm] * len(a_out),
            scratch_shapes=[
                pltpu.VMEM((ni, t), BF16), pltpu.VMEM((no, t), BF16), pltpu.VMEM((SLOTS, SUPER, t), BF16),
                pltpu.VMEM((nk, tail_cols, t), BF16), pltpu.VMEM((t, nd), BF16),
                pltpu.VMEM((nk, ni), F32), pltpu.VMEM((nk, nff), F32), pltpu.VMEM((1, no), F32),
                pltpu.VMEM((1, nd), F32),
                pltpu.VMEM((STAT_ROWS, LANES), F32), pltpu.VMEM((STAT_ROWS, LANES), F32),
                pltpu.VMEM((n_dev // 2, STAT_ROWS, LANES), F32), pltpu.VMEM((STAT_ROWS, LANES), F32),
                pltpu.VMEM((STAT_ROWS, LANES), F32), pltpu.VMEM((n_rows, LANES), F32),
                pltpu.VMEM((n_dev, 1, LANES), F32),
                dma((6,)), dma((SLOTS,)), dma((nk,)), dma((nd // CHUNK,)), dma((nk + 1,)),
                dma((ng,)), dma((ng,)), dma((ng, n_dev)), dma((ng, n_dev)), dma((n_dev,)), dma((n_dev,)),
            ],
            compiler_params=pltpu.CompilerParams(collective_id=0, has_side_effects=True,
                                                 vmem_limit_bytes=30 * 1024 * 1024),
            name="stats",
        )(x_norm.T, hid_act.T, jnp.swapaxes(dy_in, 1, 2), dy_out, w_in, w_out, row_in, col_in,
          row_out.reshape(1, no), col_out.reshape(1, nd),
          beta_two.reshape(1), rel_step.reshape(1), clip_rms.reshape(1), clip_norm.reshape(1))
        outs = [pltpu.with_memory_space_constraint(o, pltpu.VMEM) for o in outs]
        b_out = [jax.ShapeDtypeStruct(w_in.shape, F32), jax.ShapeDtypeStruct(row_in.shape, F32),
                 jax.ShapeDtypeStruct(col_in.shape, F32), jax.ShapeDtypeStruct(w_out.shape, F32),
                 jax.ShapeDtypeStruct((1, no), F32), jax.ShapeDtypeStruct((1, nd), F32)]
        wi_new, ri_new, ci_new, wo_new, ro_new, co_new = pl.pallas_call(
            update_kernel,
            out_shape=b_out,
            in_specs=[vm] * len(outs),
            out_specs=[hb, vm, vm, hb, vm, vm],
            scratch_shapes=[pltpu.VMEM((4, B_IN, nff), F32), pltpu.VMEM((2, no, CHUNK), F32), dma((4,)), dma((2,))],
            compiler_params=pltpu.CompilerParams(vmem_limit_bytes=12 * 1024 * 1024),
            name="update",
        )(*outs)
        return (wi_new, ri_new, ci_new, wo_new, ro_new.reshape(no), co_new.reshape(nd))

    in_specs = (P(None, 'tp'), P(None, 'tp'), P(), P(), P(None, 'tp', None), P('tp', None),
                P(None, 'tp'), P(), P('tp'), P(), P(), P(), P(), P())
    out_specs = (P(None, 'tp', None), P(None, 'tp'), P(), P('tp', None), P('tp'), P())
    return jax.shard_map(local_step, mesh=mesh, in_specs=in_specs, out_specs=out_specs, check_vma=False)
```

time: 149 us -> 48.2 us (0.32)
  blocking collectives: 68.8 us -> 0 us
  Pallas kernels: 0 us -> 41.4 us
  other arithmetic: 40.5 us -> 1.33 us
  matrix products: 28.5 us -> 0 us
  between operations: 8.14 us -> 3.24 us
    psum x2 -> x0, blocking collectives: 68.8 us -> none  [the longest x1 36.1 us: local_step(): totals_in = lax.psum(local_sums(grad_in, w_in, row_in), 'tp')]
    pallas_call x0 -> x2, Pallas kernels: none -> 41.4 us  [the longest x1 34.7 us: local_step(): pl.pallas_call(lambda *refs: stats_kernel(n_dev, *refs), out_shape=a_out,...]
    dot_general x2 -> x0, matrix products: 28.5 us -> none  [the longest x1 21.5 us: local_step(): jnp.einsum('ti,ktj->kij', x_norm, dy_in, preferred_element_type=jnp.float32)]
    reduce_sum x10 -> x0, other arithmetic: 22.1 us -> none  [the longest x2 8.63 us: local_sums(): w_sq = jnp.sum(weight * weight, axis=(-2, -1))[..., None]]
    sub x2 -> x0, other arithmetic: 17 us -> none  [apply_update(): return (weight - step_size * clipped, row_new, col_new)]
where the time goes in v1:
time: 48.2 us; the launch traced here: 47.9 us
  Pallas kernels  41.4 us (86%)
  between operations  3.24 us (7%)
  local copies, waits for them, and re-layouts  1.89 us (4%)
  other arithmetic  1.33 us (3%)
    pallas_call x1, Pallas kernels, local_step(): pl.pallas_call(lambda *refs: stats_kernel(n_dev, *refs), out_shape=a_out,...  34.7 us
    pallas_call x1, Pallas kernels, local_step(): pl.pallas_call(update_kernel, out_shape=b_out, in_specs=[vm] * len(outs),...  6.71 us
    pallas_call x1, other arithmetic, local_step(): pl.pallas_call(update_kernel, out_shape=b_out, in_specs=[vm] * len(outs),...  1.33 us
    reshape x1, local copies, waits for them, and re-layouts, local_step(): col_out.reshape(1, nd)  1.31 us

profile of v1, /device:TPU:0, one launch (start us, length us, event | category | flops | bytes accessed | tf_op | source)
XLA Modules:
  0.0 47.9 jit_solution(2458759763401585870)
XLA Ops:
  3.2 1.3 %reshape.37.refs_9_ = f32[1,2560]{1,0:T(1,128)} reshape(f32[2560]{0:T(1024)} %param.23) | data formatting | bytes 20480 | tf_op jit(solution)/shard_map/reshape | solution.py:466
  4.5 34.7 %stats.1 = (f32[2,160,6720]{2,1,0:T(8,128)S(1)}, f32[420,2560]{1,0:T(8,128)S(1)}, f32[2,160,6720]{2,1,0:T(8,128)S(1)}, f32[420,2560]{1,0:T(8,128)S(1)}, f32[744,...) custom-call(bf16[160,1024]{1,0:T(8,128)(2,1)} %bitcast.15, ...), custom_call_target="tpu_custom_call" | custom-call | tf_op jit(solution)/shard_map/stats/pallas_call | solution.py:445
  39.3 6.7 %update.1 = (f32[2,160,6720]{2,1,0:T(8,128)}, f32[2,160]{1,0:T(2,128)}, f32[2,6720]{1,0:T(2,128)}, f32[420,2560]{1,0:T(8,128)}, f32[1,420]{1,0:T(1,128)}, /*index=5*/f32[1,2560]{1,0:T(1,128)S(1)}) custom-call(f32[2,160,6720]{2,1,0:T(8,128)S(1)} %get-tuple-element.20.di, f32[420,2560]{1,0:T(8,128)S(1)} %get-tuple-element.21.do, ...), custom_call_target="tpu_custom_call" | custom-call | tf_op jit(solution)/shard_map/update/pallas_call | solution.py:472
  46.0 0.0 copy-start
  46.0 0.6 %copy-done = f32[1,2560]{1,0:T(1,128)} copy-done((f32[1,2560]{1,0:T(1,128)}, f32[1,2560]{1,0:T(1,128)S(1)}, u32[]{:S(2)}) %copy-start) | copy-done | bytes 10264
  46.6 1.3 %reduce = f32[2560]{0:T(1024)} reduce(f32[1,2560]{1,0:T(1,128)} %copy-done, f32[]{:T(128)} %constant.3), dimensions={0}, to_apply=%get-tuple-element.33.reduce_sub_computation | reduce | bytes 20484 | tf_op jit(solution)/shard_map/update/pallas_call | solution.py:472
Async XLA Ops:
  46.0 0.6 %copy-start = (f32[1,2560]{1,0:T(1,128)}, f32[1,2560]{1,0:T(1,128)S(1)}, u32[]{:S(2)}) copy-start(f32[1,2560]{1,0:T(1,128)S(1)} %get-tuple-element.33) | copy-start | bytes 30724

commit v2 on v0

v2 whole, which is shorter than its diff:
```python
import jax
import jax.numpy as jnp
from jax import lax
from jax.experimental import pallas as pl
from jax.experimental.pallas import tpu as pltpu
from jax.sharding import PartitionSpec as P

MESH = pl.DeviceIdType.MESH
EPS_ONE = 1e-30
EPS_TWO = 1e-3
LANES = 128
F32 = jnp.float32
BF16 = jnp.bfloat16

OUT_ROW, IN_ROW, IN_STEP, STAT_ROWS = 0, 32, 64, 160
SCALAR_ROW = 24
STAGED = ((0, 32), (32, 64), (128, 32))
DIRECT_ROW = 96
DIRECT = ((112, 16), (96, 8), (104, 8))
CHUNK = 512
SUPER = 2048
HALF = 1024
SLOTS = 4
SCOPED = 30 * 1024 * 1024
PIECE = 256


def scope(name):
    pass


def lane_to_column(vec, rows):
    n = vec.shape[1]
    r = lax.broadcasted_iota(jnp.int32, (rows, n), 0)
    c = lax.broadcasted_iota(jnp.int32, (rows, n), 1)
    col = jnp.sum(jnp.where(r == c, jnp.broadcast_to(vec, (rows, n)), 0.0), axis=1, keepdims=True)
    full = jnp.broadcast_to(col, (rows, LANES))
    if rows > n:
        full = jnp.where(lax.broadcasted_iota(jnp.int32, (rows, LANES), 0) < n, full, 1.0)
    return full


def column_to_lane(col, n):
    part = col[:, :n]
    r = lax.broadcasted_iota(jnp.int32, part.shape, 0)
    c = lax.broadcasted_iota(jnp.int32, part.shape, 1)
    return jnp.sum(jnp.where(r == c, part, 0.0), axis=0, keepdims=True)


def total(x):
    return jnp.sum(jnp.sum(x, axis=0, keepdims=True), axis=1, keepdims=True)


def stats_kernel(n_dev, x_hbm, h_hbm, dyo_hbm, dyi_hbm, wi_hbm, wo_hbm, ri_hbm, ci_hbm, ro_hbm, co_hbm,
                 beta_s, rel_s, crms_s, cnorm_s,
                 di, do, wi, wo, rcol, acol, cnew, bden, kout,
                 x_v, h_v, dyo_v, ring, tail, ri_v, ci_v, ro_v, co_v, part, pair, tot, recv, recv_all, cden, rsum, recv2,
                 in_sem, dyo_sem, ring_sem, tail_sem, w_sem, pair_sem, chip_sem, back_sem, all_sem, two_sem):
    me = lax.axis_index('tp')
    core = lax.rem(me, 2)
    chip = me // 2
    partner = me + 1 - 2 * core
    nk, ni, nff = di.shape
    no, nd = wo.shape
    no_pad = -(-no // 8) * 8
    n_super = nff // SUPER
    tail_cols = nff - n_super * SUPER
    rows_in, rows_out = ni * n_dev, no * n_dev
    n_chip = n_dev // 2

    barrier = pltpu.get_barrier_semaphore()
    for d in range(1, n_dev):
        pl.semaphore_signal(barrier, inc=1, device_id=(lax.rem(me + d, n_dev),), device_id_type=MESH)

    scope("init")
    sequence = [(0, c) for c in range(n_super)] + [(1, c) for c in range(n_super - 1, -1, -1)]

    def half_copy(i, p):
        k, c = sequence[i]
        return pltpu.make_async_copy(dyi_hbm.at[k, pl.ds(c * SUPER + p * HALF, HALF), :],
                                     ring.at[i % SLOTS, pl.ds(p * HALF, HALF), :], ring_sem.at[i % SLOTS, p])

    def super_start(i):
        half_copy(i, 0).start()
        half_copy(i, 1).start()

    def super_wait(i):
        half_copy(i, 0).wait()
        half_copy(i, 1).wait()

    tail_cp = [pltpu.make_async_copy(dyi_hbm.at[k, pl.ds(n_super * SUPER, tail_cols), :], tail.at[k], tail_sem.at[k])
               for k in range(nk)]
    w_cp = [pltpu.make_async_copy(wi_hbm.at[k], wi.at[k], w_sem.at[k]) for k in range(nk)]
    w_cp.append(pltpu.make_async_copy(wo_hbm, wo, w_sem.at[nk]))
    small = [pltpu.make_async_copy(a, b, in_sem.at[i]) for i, (a, b) in enumerate(
        ((ro_hbm, ro_v), (ri_hbm, ri_v), (co_hbm, co_v), (ci_hbm, ci_v), (h_hbm, h_v), (x_hbm, x_v)))]
    dyo_cp = [pltpu.make_async_copy(dyo_hbm.at[:, pl.ds(c, CHUNK)], dyo_v.at[:, pl.ds(c, CHUNK)],
                                    dyo_sem.at[c // CHUNK]) for c in range(0, nd, CHUNK)]
    for cp in small[4:5] + dyo_cp[:2]:
        cp.start()
    part[...] = jnp.zeros_like(part)
    rsum[...] = jnp.zeros_like(rsum)

    def halves(start, size, c):
        return pl.ds(pl.multiple_of(start + c * (size // 2), 8), size // 2)

    def remote(src, dst, sem, device):
        return pltpu.make_async_remote_copy(src_ref=src, dst_ref=dst, send_sem=sem.at[0], recv_sem=sem.at[1],
                                            device_id=(device,), device_id_type=MESH)

    def pair_copy(g):
        rows = halves(*STAGED[g], 1 - core)
        return remote(part.at[rows, :], pair.at[rows, :], pair_sem.at[g], partner)

    def chip_copy(g, d):
        ref = recv.at[chip, halves(*STAGED[g], core), :]
        return remote(ref, ref, chip_sem.at[g], lax.rem(me + 2 * d, n_dev))

    def back_copy(g):
        ref = tot.at[halves(*STAGED[g], core), :]
        return remote(ref, ref, back_sem.at[g], partner)

    def all_copy(g, d):
        start, size = DIRECT[g]
        ref = recv_all.at[me, pl.ds(start - DIRECT_ROW, size), :]
        return remote(ref, ref, all_sem.at[g], lax.rem(me + d, n_dev))

    def two_copy(d):
        return remote(recv2.at[me], recv2.at[me], two_sem, lax.rem(me + d, n_dev))

    def bytes_of(ref, sem):
        pltpu.make_async_copy(ref, ref, sem).wait()

    def chip_stage(g):
        rows = halves(*STAGED[g], core)
        pair_copy(g).wait_recv()
        recv[chip, rows, :] = part[rows, :] + pair[rows, :]
        for d in range(1, n_chip):
            chip_copy(g, d).start()

    def back_stage(g):
        start, size = STAGED[g]
        rows = halves(start, size, core)
        bytes_of(recv.at[pl.ds(0, n_chip - 1), rows, :], chip_sem.at[g, 1])
        t = recv[0, rows, :]
        for c in range(1, n_chip):
            t = t + recv[c, rows, :]
        tot[rows, :] = t
        back_copy(g).start()

    def direct_stage(g):
        start, size = DIRECT[g]
        rows = pl.ds(start - DIRECT_ROW, size)
        recv_all[me, rows, :] = part[pl.ds(start, size), :]
        for d in range(1, n_dev):
            all_copy(g, d).start()

    def square_sums(g, row0, stat0):
        m, n = g.shape
        sq = g * g
        cols = jnp.sum(sq, axis=0, keepdims=True)
        acc = rsum[pl.ds(row0, m), :]
        for b in range(0, n, LANES):
            w = min(LANES, n - b)
            if w == LANES:
                acc += sq[:, b:b + w]
                part[pl.ds(stat0 + b // LANES, 1), :] = cols[:, b:b + w]
            else:
                acc = acc + jnp.concatenate([sq[:, b:b + w], jnp.zeros((m, LANES - w), F32)], axis=1)
                part[pl.ds(stat0 + b // LANES, 1), pl.ds(0, w)] = cols[:, b:b + w]
        rsum[pl.ds(row0, m), :] = acc

    def nt(dy):
        return lax.dot_general(dy, x_v[...], (((1,), (1,)), ((), ())), preferred_element_type=F32).T

    def in_piece(k, col, dy):
        g = nt(dy)
        di[k, :, pl.ds(col, g.shape[1])] = g
        square_sums(g, k * ni, IN_ROW + IN_STEP * k + col // LANES)

    def super_step(i, start=0, stop=SUPER):
        k, c = sequence[i]
        for p in range(start, stop, PIECE):
            in_piece(k, c * SUPER + p, ring[i % SLOTS, pl.ds(p, PIECE), :])

    def tail_step(k):
        for p in range(0, tail_cols, 256):
            in_piece(k, n_super * SUPER + p, tail[k, pl.ds(p, min(256, tail_cols - p)), :])

    def out_piece(start, stop):
        for col in range(start, stop, 256):
            g = jnp.dot(h_v[...], dyo_v[:, pl.ds(col, 256)], preferred_element_type=F32)
            do[:, pl.ds(col, 256)] = g
            square_sums(g, nk * ni, OUT_ROW + col // LANES)

    scope("out")
    small[4].wait()
    dyo_cp[0].wait()
    for cp in dyo_cp[2:4]:
        cp.start()
    out_piece(0, CHUNK)
    dyo_cp[1].wait()
    for cp in dyo_cp[4:] + small[5:6] + small[:4]:
        cp.start()
    half_copy(0, 0).start()
    scope("out1")
    dyo_cp[2].wait()
    out_piece(CHUNK, 3 * CHUNK)
    half_copy(0, 1).start()
    super_start(1)
    scope("out2")
    for cp in dyo_cp[3:]:
        cp.wait()
    out_piece(3 * CHUNK, nd)
    for cp in small[:2]:
        cp.wait()
    lane = lax.broadcasted_iota(jnp.int32, (1, LANES), 1)
    row_sums = jnp.where(lane == 2, jnp.sum(ro_v[...], axis=1, keepdims=True), 0.0)
    for k in range(nk):
        row_sums += jnp.where(lane == k, jnp.sum(ri_v[pl.ds(k, 1), :], axis=1, keepdims=True), 0.0)
    part[pl.ds(SCALAR_ROW, 1), :] = row_sums
    pl.semaphore_wait(barrier, n_dev - 1)
    pair_copy(0).start()

    scope("in0")
    small[5].wait()
    super_wait(0)
    super_start(2)
    tail_cp[0].start()
    super_step(0)
    chip_stage(0)
    scope("in1")
    super_wait(1)
    super_start(3)
    tail_cp[1].start()
    super_step(1)
    scope("in2")
    super_wait(2)
    tail_cp[0].wait()
    super_start(4)
    super_step(2)
    tail_step(0)
    pair_copy(1).start()
    scope("in3")
    super_wait(3)
    tail_cp[1].wait()
    super_start(5)
    super_step(3)
    tail_step(1)
    pair_copy(2).start()
    chip_stage(1)
    scope("in4")
    super_wait(4)
    super_step(4)
    direct_stage(0)
    chip_stage(2)
    scope("in5")
    super_wait(5)
    for cp in w_cp:
        cp.start()
    super_step(5, 0, HALF)
    direct_stage(1)
    super_step(5, HALF, SUPER)
    direct_stage(2)
    back_stage(0)

    scope("forms")
    for cp in small[2:4]:
        cp.wait()
    cden[...] = jnp.ones_like(cden)
    cden[pl.ds(OUT_ROW, nd // LANES), :] = co_v[...]
    for k in range(nk):
        for q in range(nff // LANES):
            cden[pl.ds(IN_ROW + IN_STEP * k + q, 1), :] = ci_v[pl.ds(k, 1), pl.ds(q * LANES, LANES)]
        rest = nff % LANES
        if rest:
            cden[pl.ds(IN_ROW + IN_STEP * k + nff // LANES, 1), pl.ds(0, rest)] = (
                ci_v[pl.ds(k, 1), pl.ds(nff - rest, rest)])
    for k in range(nk):
        vec = ri_v[pl.ds(k, 1), :]
        for p in range(0, ni, LANES):
            n = min(LANES, ni - p)
            rcol[pl.ds(k * ni + p, n), :] = lane_to_column(vec[:, p:p + n], n)
    vec = ro_v[...]
    for p in range(0, no, LANES):
        n = min(LANES, no - p)
        rows = -(-n // 8) * 8
        rcol[pl.ds(nk * ni + p, rows), :] = lane_to_column(vec[:, p:p + n], rows)
    rsum[...] = jnp.broadcast_to(jnp.sum(rsum[...], axis=1, keepdims=True), rsum.shape)
    back_stage(1)

    def w_square_in(k):
        def body(q, acc):
            w = wi[k, :, pl.ds(pl.multiple_of(q * LANES, LANES), LANES)]
            return acc + w * w
        acc = lax.fori_loop(0, nff // LANES, body, jnp.zeros((ni, LANES), F32), unroll=4)
        rest = nff % LANES
        w = wi[k, :, pl.ds(nff - rest, rest)]
        return total(acc) + total(w * w)

    def w_square_out():
        m = no // 8 * 8
        acc = jnp.zeros((8, nd), F32)
        acc = lax.fori_loop(0, m // 8, lambda i, a: a + jnp.square(wo[pl.ds(pl.multiple_of(i * 8, 8), 8), :]), acc,
                            unroll=4)
        w = wo[pl.ds(m, no - m), :]
        return total(acc) + total(w * w)

    scope("wsq")
    w_sq = []
    for k in range(nk):
        w_cp[k].wait()
        w_sq.append(w_square_in(k))
    scope("back2")
    back_stage(2)
    scope("wsq2")
    w_cp[nk].wait()
    w_sq.append(w_square_out())

    scope("wait1")
    for g in range(len(STAGED)):
        ref = tot.at[halves(*STAGED[g], 1 - core), :]
        bytes_of(ref, back_sem.at[g, 1])
    for g in range(len(DIRECT)):
        start, size = DIRECT[g]
        rows = pl.ds(start - DIRECT_ROW, size)
        bytes_of(recv_all.at[pl.ds(0, n_dev - 1), rows, :], all_sem.at[g, 1])
    t = recv_all[0]
    for c in range(1, n_dev):
        t = t + recv_all[c]
    tot[pl.ds(DIRECT_ROW, t.shape[0]), :] = t

    scope("stats")
    beta = jnp.full((1, 1), beta_s[()], F32)
    mix = 1.0 - beta
    seg = [(IN_ROW + IN_STEP * k, IN_STEP, k * ni, ni, rows_in, nff) for k in range(nk)]
    seg.append((OUT_ROW, SCALAR_ROW, nk * ni, no_pad, rows_out, nd))
    sums = [total(tot[pl.ds(a, n), :]) for a, n, *_ in seg]
    norm_sq = sums[0] + sums[1] + sums[2]
    scale = jnp.minimum(1.0, jnp.full((1, 1), cnorm_s[()], F32) / jnp.sqrt(norm_sq))
    row_tot = tot[pl.ds(SCALAR_ROW, 1), :]
    for j, (a, n, ra, rn, m_all, n_all) in enumerate(seg):
        c2 = beta * cden[pl.ds(a, n), :] + mix * (scale * (scale * tot[pl.ds(a, n), :]) * (1.0 / m_all) + EPS_ONE)
        cnew[pl.ds(a, n), :] = c2
        bden[pl.ds(a, n), :] = scale * lax.rsqrt(c2)
        r2 = beta * rcol[pl.ds(ra, rn), :] + mix * (scale * (scale * rsum[pl.ds(ra, rn), :]) * (1.0 / n_all) + EPS_ONE)
        rcol[pl.ds(ra, rn), :] = r2
        r_all = jnp.sum(jnp.where(lane == j, row_tot, 0.0), axis=1, keepdims=True)
        level = beta * (r_all / m_all) + mix * (scale * (scale * (sums[j] / n_all)) * (1.0 / m_all) + EPS_ONE)
        acol[pl.ds(ra, rn), :] = lax.rsqrt(r2 / level)

    def u_square(ref, k, row0, m, cols, stat0, arow):
        rows = pl.ds(row0, m)

        def block(col, w, brow):
            idx = (rows, pl.ds(col, w)) if k is None else (k, rows, pl.ds(col, w))
            t = ref[idx] * jnp.broadcast_to(bden[pl.ds(brow, 1), pl.ds(0, w)], (m, w))
            return t * t

        def body(i, acc):
            for q in range(4):
                col = pl.multiple_of(i * 4 * LANES + q * LANES, LANES)
                acc = acc + block(col, LANES, stat0 + i * 4 + q)
            return acc
        acc = lax.fori_loop(0, cols // LANES // 4, body, jnp.zeros((m, LANES), F32))
        a = acol[pl.ds(arow, m), :]
        u = total(acc * a * a)
        rest = cols % LANES
        if rest:
            a = acol[pl.ds(arow, m), pl.ds(0, rest)]
            u = u + total(block(cols - rest, rest, stat0 + cols // LANES) * a * a)
        return u

    scope("upass")
    u_sq = [u_square(di, k, 0, ni, nff, IN_ROW + IN_STEP * k, k * ni) for k in range(nk)]
    u_sq.append(sum(u_square(do, None, row0, m, nd, OUT_ROW, nk * ni + row0)
                    for row0, m in ((0, 144), (144, 144), (288, no - 288))))

    scope("x2")
    msg = jnp.zeros((1, LANES), F32)
    for j in range(3):
        msg = msg + jnp.where(lane == j, u_sq[j], 0.0) + jnp.where(lane == 3 + j, w_sq[j], 0.0)
    recv2[me] = msg
    for d in range(1, n_dev):
        two_copy(d).start()
    for g in range(len(STAGED)):
        pair_copy(g).wait_send()
        back_copy(g).wait_send()
        bytes_of(recv.at[pl.ds(0, n_chip - 1), halves(*STAGED[g], core), :], chip_sem.at[g, 0])
    for g in range(len(DIRECT)):
        start, size = DIRECT[g]
        bytes_of(recv_all.at[pl.ds(0, n_dev - 1), pl.ds(start - DIRECT_ROW, size), :], all_sem.at[g, 0])
    bytes_of(recv2.at[pl.ds(0, n_dev - 1)], two_sem.at[1])
    scope("fin")
    all_sums = recv2[0]
    for c in range(1, n_dev):
        all_sums = all_sums + recv2[c]
    for j, (_, _, _, _, m_all, n_all) in enumerate(seg):
        u = jnp.sum(jnp.where(lane == j, all_sums, 0.0), axis=1, keepdims=True)
        w = jnp.sum(jnp.where(lane == 3 + j, all_sums, 0.0), axis=1, keepdims=True)
        u_rms = jnp.sqrt(u / (m_all * n_all))
        w_rms = jnp.sqrt(w / (m_all * n_all))
        step_size = jnp.full((1, 1), rel_s[()], F32) * jnp.maximum(EPS_TWO, w_rms)
        k = step_size / jnp.maximum(1.0, u_rms / jnp.full((1, 1), crms_s[()], F32))
        kout[pl.ds(j, 1), :] = jnp.broadcast_to(k, (1, LANES))
    bytes_of(recv2.at[pl.ds(0, n_dev - 1)], two_sem.at[0])
    scope(None)


B_IN = 32


def update_kernel(di, do, wi, wo, rcol, acol, cnew, bden, kout, wi_out, ri_out, ci_out, wo_out, ro_out, co_out,
                  buf_in, buf_out, sem_in, sem_out):
    nk, ni, nff = di.shape
    no, nd = do.shape
    steps = ni // B_IN

    def in_copy(k, i, slot):
        return pltpu.make_async_copy(buf_in.at[slot], wi_out.at[k, pl.ds(i * B_IN, B_IN), :], sem_in.at[slot])

    def widths(n):
        return [(c, min(LANES, n - c)) for c in range(0, n, LANES)]

    def step_of(w, g, b, a, kk):
        return w - kk * ((g * jnp.broadcast_to(b, g.shape)) * a)

    pend = [None] * buf_in.shape[0]
    for k in range(nk):
        kk = jnp.broadcast_to(kout[pl.ds(k, 1), :], (B_IN, LANES))
        for i in range(steps):
            slot = (k * steps + i) % buf_in.shape[0]
            if pend[slot] is not None:
                pend[slot].wait()
            a = acol[pl.ds(k * ni + i * B_IN, B_IN), :]
            rows = pl.ds(i * B_IN, B_IN)
            for q, (c, n) in enumerate(widths(nff)):
                cc = pl.ds(c, n)
                b = bden[pl.ds(IN_ROW + IN_STEP * k + q, 1), pl.ds(0, n)]
                buf_in[slot, :, cc] = step_of(wi[k, rows, cc], di[k, rows, cc], b, a[:, :n], kk[:, :n])
            cp = in_copy(k, i, slot)
            cp.start()
            pend[slot] = cp
    pend_out = [None] * buf_out.shape[0]
    for i in range(nd // CHUNK):
        slot = i % buf_out.shape[0]
        if pend_out[slot] is not None:
            pend_out[slot].wait()
        kk = jnp.broadcast_to(kout[pl.ds(nk, 1), :], (40, LANES))
        bs = [bden[pl.ds(OUT_ROW + i * (CHUNK // LANES) + q, 1), :] for q in range(CHUNK // LANES)]

        def rows_of(o, n, i=i, slot=slot, kk=kk, bs=bs):
            r = pl.ds(o, n)
            a = acol[pl.ds(nk * ni + o, n), :]
            for q, b in enumerate(bs):
                cc = pl.ds(i * CHUNK + q * LANES, LANES)
                buf_out[slot, r, pl.ds(q * LANES, LANES)] = step_of(wo[r, cc], do[r, cc], b, a, kk[:n])

        for o in range(0, no, 40):
            rows_of(o, min(40, no - o))
        cp = pltpu.make_async_copy(buf_out.at[slot], wo_out.at[:, pl.ds(i * CHUNK, CHUNK)], sem_out.at[slot])
        cp.start()
        pend_out[slot] = cp
    co_out[...] = cnew[pl.ds(OUT_ROW, nd // LANES), :]
    for k in range(nk):
        for c, n in widths(nff):
            ci_out[pl.ds(k, 1), pl.ds(c, n)] = cnew[pl.ds(IN_ROW + IN_STEP * k + c // LANES, 1), pl.ds(0, n)]
        for c, n in widths(ni):
            ri_out[pl.ds(k, 1), pl.ds(c, n)] = column_to_lane(rcol[pl.ds(k * ni + c, n), :], n)
    for c, n in widths(no):
        ro_out[:, pl.ds(c, n)] = column_to_lane(rcol[pl.ds(nk * ni + c, -(-n // 8) * 8), :], n)
    for cp in pend + pend_out:
        if cp is not None:
            cp.wait()


def solution(mesh):
    n_dev = mesh.shape['tp']

    def local_step(x_norm, hid_act, dy_in, dy_out, w_in, w_out, row_in, col_in, row_out, col_out,
                   beta_two, rel_step, clip_rms, clip_norm):
        t, ni = x_norm.shape
        no = hid_act.shape[1]
        nk, _, nff = dy_in.shape
        nd = dy_out.shape[1]
        no_pad = -(-no // 8) * 8
        tail_cols = nff - nff // SUPER * SUPER
        vm = pl.BlockSpec(memory_space=pltpu.VMEM)
        hb = pl.BlockSpec(memory_space=pltpu.HBM)
        sm = pl.BlockSpec(memory_space=pltpu.SMEM)
        dma = pltpu.SemaphoreType.DMA
        n_rows = nk * ni + no_pad
        a_out = [pltpu.VMEM((nk, ni, nff), F32), pltpu.VMEM((no, nd), F32),
                 pltpu.VMEM((nk, ni, nff), F32), pltpu.VMEM((no, nd), F32),
                 pltpu.VMEM((n_rows, LANES), F32), pltpu.VMEM((n_rows, LANES), F32),
                 pltpu.VMEM((STAT_ROWS, LANES), F32), pltpu.VMEM((STAT_ROWS, LANES), F32),
                 pltpu.VMEM((8, LANES), F32)]
        ns, ng = len(STAGED), len(DIRECT)
        stat = pltpu.VMEM((STAT_ROWS, LANES), F32)
        outs = pl.pallas_call(
            lambda *refs: stats_kernel(n_dev, *refs),
            out_shape=a_out,
            in_specs=[hb] * 10 + [sm] * 4,
            out_specs=[vm] * len(a_out),
            scratch_shapes=[
                pltpu.VMEM((ni, t), BF16), pltpu.VMEM((no, t), BF16), pltpu.VMEM((t, nd), BF16),
                pltpu.VMEM((SLOTS, SUPER, t), BF16), pltpu.VMEM((nk, tail_cols, t), BF16),
                pltpu.VMEM((nk, ni), F32), pltpu.VMEM((nk, nff), F32), pltpu.VMEM((1, no), F32),
                pltpu.VMEM((nd // LANES, LANES), F32),
                stat, stat, stat, pltpu.VMEM((n_dev // 2, STAT_ROWS, LANES), F32),
                pltpu.VMEM((n_dev, sum(n for _, n in DIRECT), LANES), F32), stat,
                pltpu.VMEM((n_rows, LANES), F32), pltpu.VMEM((n_dev, 1, LANES), F32),
                dma((6,)), dma((nd // CHUNK,)), dma((SLOTS, 2)), dma((nk,)), dma((nk + 1,)),
                dma((ns, 2)), dma((ns, 2)), dma((ns, 2)), dma((ng, 2)), dma((2,)),
            ],
            compiler_params=pltpu.CompilerParams(collective_id=0, has_side_effects=True,
                                                 vmem_limit_bytes=SCOPED),
            name="stats",
        )(x_norm.T, hid_act.T, dy_out, jnp.swapaxes(dy_in, 1, 2), w_in, w_out, row_in, col_in,
          row_out.reshape(1, no), col_out.reshape(nd // LANES, LANES),
          beta_two, rel_step, clip_rms, clip_norm)
        outs = [pltpu.with_memory_space_constraint(o, pltpu.VMEM) for o in outs]
        b_out = [jax.ShapeDtypeStruct(w_in.shape, F32), jax.ShapeDtypeStruct(row_in.shape, F32),
                 jax.ShapeDtypeStruct(col_in.shape, F32), jax.ShapeDtypeStruct(w_out.shape, F32),
                 jax.ShapeDtypeStruct((1, no), F32), jax.ShapeDtypeStruct((nd // LANES, LANES), F32)]
        wi_new, ri_new, ci_new, wo_new, ro_new, co_new = pl.pallas_call(
            update_kernel,
            out_shape=b_out,
            in_specs=[vm] * len(outs),
            out_specs=[hb, vm, vm, hb, vm, vm],
            scratch_shapes=[pltpu.VMEM((4, B_IN, nff), F32), pltpu.VMEM((2, no, CHUNK), F32), dma((4,)), dma((2,))],
            compiler_params=pltpu.CompilerParams(vmem_limit_bytes=SCOPED),
            name="update",
        )(*outs)
        return (wi_new, ri_new, ci_new, wo_new, ro_new.reshape(no), co_new.reshape(nd))

    in_specs = (P(None, 'tp'), P(None, 'tp'), P(), P(), P(None, 'tp', None), P('tp', None),
                P(None, 'tp'), P(), P('tp'), P(), P(), P(), P(), P())
    out_specs = (P(None, 'tp', None), P(None, 'tp'), P(), P('tp', None), P('tp'), P())
    return jax.shard_map(local_step, mesh=mesh, in_specs=in_specs, out_specs=out_specs, check_vma=False)
```

time: 149 us -> 38.2 us (0.26)
  blocking collectives: 68.8 us -> 0 us
  other arithmetic: 40.5 us -> 0 us
  Pallas kernels: 0 us -> 34.6 us
  matrix products: 28.5 us -> 0 us
  between operations: 8.14 us -> 3.39 us
  local copies, waits for them, and re-layouts: 2.39 us -> 0 us
    psum x2 -> x0, blocking collectives: 68.8 us -> none  [the longest x1 36.1 us: local_step(): totals_in = lax.psum(local_sums(grad_in, w_in, row_in), 'tp')]
    pallas_call x0 -> x2, Pallas kernels: none -> 34.6 us  [the longest x1 28.3 us: local_step(): pl.pallas_call(lambda *refs: stats_kernel(n_dev, *refs), out_shape=a_out,...]
    dot_general x2 -> x0, matrix products: 28.5 us -> none  [the longest x1 21.5 us: local_step(): jnp.einsum('ti,ktj->kij', x_norm, dy_in, preferred_element_type=jnp.float32)]
    reduce_sum x10 -> x0, other arithmetic: 22.1 us -> none  [the longest x2 8.63 us: local_sums(): w_sq = jnp.sum(weight * weight, axis=(-2, -1))[..., None]]
    sub x2 -> x0, other arithmetic: 17 us -> none  [apply_update(): return (weight - step_size * clipped, row_new, col_new)]
where the time goes in v2:
time: 38.2 us; the launch traced here: 38 us
  Pallas kernels  34.6 us (91%)
  between operations  3.39 us (9%)
    pallas_call x1, Pallas kernels, local_step(): pl.pallas_call(lambda *refs: stats_kernel(n_dev, *refs), out_shape=a_out,...  28.3 us
    pallas_call x1, Pallas kernels, local_step(): pl.pallas_call(update_kernel, out_shape=b_out, in_specs=[vm] * len(outs),...  6.3 us

profile of v2, /device:TPU:0, one launch (start us, length us, event | category | flops | bytes accessed | tf_op | source)
XLA Modules:
  0.0 38.0 jit_solution(4594272466252687857)
XLA Ops:
  3.2 28.3 %stats.1 = (f32[2,160,6720]{2,1,0:T(8,128)S(1)}, f32[420,2560]{1,0:T(8,128)S(1)}, f32[2,160,6720]{2,1,0:T(8,128)S(1)}, f32[420,2560]{1,0:T(8,128)S(1)}, f32[744,...) custom-call(bf16[160,1024]{1,0:T(8,128)(2,1)} %bitcast.9, ...), custom_call_target="tpu_custom_call" | custom-call | tf_op jit(solution)/shard_map/stats/pallas_call | solution.py:500
  31.5 6.3 %update.1 = (f32[2,160,6720]{2,1,0:T(8,128)}, f32[2,160]{1,0:T(2,128)}, f32[2,6720]{1,0:T(2,128)}, f32[420,2560]{1,0:T(8,128)}, f32[1,420]{1,0:T(1,128)}, /*index=5*/f32[20,128]{1,0:T(8,128)}) custom-call(f32[2,160,6720]{2,1,0:T(8,128)S(1)} %get-tuple-element.21.di, f32[420,2560]{1,0:T(8,128)S(1)} %get-tuple-element.22.do, ...), custom_call_target="tpu_custom_call" | custom-call | tf_op jit(solution)/shard_map/update/pallas_call | solution.py:526

commit v3 on v2

--- a/solution.py
+++ b/solution.py
@@ -14,9 +14,9 @@
 
 OUT_ROW, IN_ROW, IN_STEP, STAT_ROWS = 0, 32, 64, 160
 SCALAR_ROW = 24
-STAGED = ((0, 32), (32, 64), (128, 32))
+STAGED = ((0, 32), (32, 64), (128, 32), (112, 16))
 DIRECT_ROW = 96
-DIRECT = ((112, 16), (96, 8), (104, 8))
+DIRECT = ((96, 8), (104, 8))
 CHUNK = 512
 SUPER = 2048
 HALF = 1024
@@ -54,7 +54,7 @@
 def stats_kernel(n_dev, x_hbm, h_hbm, dyo_hbm, dyi_hbm, wi_hbm, wo_hbm, ri_hbm, ci_hbm, ro_hbm, co_hbm,
                  beta_s, rel_s, crms_s, cnorm_s,
                  di, do, wi, wo, rcol, acol, cnew, bden, kout,
-                 x_v, h_v, dyo_v, ring, tail, ri_v, ci_v, ro_v, co_v, part, pair, tot, recv, recv_all, cden, rsum, recv2,
+                 x_v, h_v, dyo_v, ring, tail, raw, ri_v, ci_v, ro_v, co_v, part, pair, tot, recv, recv_all, cden, rsum, recv2,
                  in_sem, dyo_sem, ring_sem, tail_sem, w_sem, pair_sem, chip_sem, back_sem, all_sem, two_sem):
     me = lax.axis_index('tp')
     core = lax.rem(me, 2)
@@ -170,28 +170,46 @@
                 part[pl.ds(stat0 + b // LANES, 1), pl.ds(0, w)] = cols[:, b:b + w]
         rsum[pl.ds(row0, m), :] = acc
 
-    def nt(dy):
-        return lax.dot_general(dy, x_v[...], (((1,), (1,)), ((), ())), preferred_element_type=F32).T
-
-    def in_piece(k, col, dy):
-        g = nt(dy)
+    deferred = []
+
+    def flush():
+        for f in deferred:
+            f()
+        deferred.clear()
+
+    def finish_in(k, col, g):
+        g = g.T
         di[k, :, pl.ds(col, g.shape[1])] = g
         square_sums(g, k * ni, IN_ROW + IN_STEP * k + col // LANES)
 
-    def super_step(i, start=0, stop=SUPER):
+    def finish_out(col):
+        square_sums(do[:, pl.ds(col, 256)], nk * ni, OUT_ROW + col // LANES)
+
+    def in_block(pieces, defer):
+        for j, (k, col, n, ref) in enumerate(pieces):
+            g = lax.dot_general(ref[...], x_v[...], (((1,), (1,)), ((), ())), preferred_element_type=F32)
+            slot = j - len(pieces) + 2
+            if defer and slot >= 0:
+                raw[slot, pl.ds(0, n), :] = g
+                deferred.append(lambda k=k, col=col, n=n, slot=slot: finish_in(k, col, raw[slot, pl.ds(0, n), :]))
+            else:
+                finish_in(k, col, g)
+
+    def super_pieces(i, start=0, stop=SUPER):
         k, c = sequence[i]
-        for p in range(start, stop, PIECE):
-            in_piece(k, c * SUPER + p, ring[i % SLOTS, pl.ds(p, PIECE), :])
-
-    def tail_step(k):
-        for p in range(0, tail_cols, 256):
-            in_piece(k, n_super * SUPER + p, tail[k, pl.ds(p, min(256, tail_cols - p)), :])
+        return [(k, c * SUPER + p, 256, ring.at[i % SLOTS, pl.ds(p, 256), :]) for p in range(start, stop, 256)]
+
+    def tail_pieces(k):
+        return [(k, n_super * SUPER + p, min(256, tail_cols - p), tail.at[k, pl.ds(p, min(256, tail_cols - p)), :])
+                for p in range(0, tail_cols, 256)]
 
     def out_piece(start, stop):
         for col in range(start, stop, 256):
-            g = jnp.dot(h_v[...], dyo_v[:, pl.ds(col, 256)], preferred_element_type=F32)
-            do[:, pl.ds(col, 256)] = g
-            square_sums(g, nk * ni, OUT_ROW + col // LANES)
+            do[:, pl.ds(col, 256)] = jnp.dot(h_v[...], dyo_v[:, pl.ds(col, 256)], preferred_element_type=F32)
+            if col + 512 >= stop:
+                deferred.append(lambda col=col: finish_out(col))
+            else:
+                finish_out(col)
 
     scope("out")
     small[4].wait()
@@ -205,12 +223,14 @@
     half_copy(0, 0).start()
     scope("out1")
     dyo_cp[2].wait()
+    flush()
     out_piece(CHUNK, 3 * CHUNK)
     half_copy(0, 1).start()
     super_start(1)
     scope("out2")
     for cp in dyo_cp[3:]:
         cp.wait()
+    flush()
     out_piece(3 * CHUNK, nd)
     for cp in small[:2]:
         cp.wait()
@@ -219,49 +239,51 @@
     for k in range(nk):
         row_sums += jnp.where(lane == k, jnp.sum(ri_v[pl.ds(k, 1), :], axis=1, keepdims=True), 0.0)
     part[pl.ds(SCALAR_ROW, 1), :] = row_sums
-    pl.semaphore_wait(barrier, n_dev - 1)
-    pair_copy(0).start()
-
     scope("in0")
     small[5].wait()
     super_wait(0)
     super_start(2)
     tail_cp[0].start()
-    super_step(0)
-    chip_stage(0)
+    flush()
+    in_block(super_pieces(0), True)
+    pl.semaphore_wait(barrier, n_dev - 1)
+    pair_copy(0).start()
     scope("in1")
     super_wait(1)
     super_start(3)
     tail_cp[1].start()
-    super_step(1)
+    flush()
+    in_block(super_pieces(1), True)
+    chip_stage(0)
     scope("in2")
     super_wait(2)
     tail_cp[0].wait()
     super_start(4)
-    super_step(2)
-    tail_step(0)
+    flush()
+    in_block(super_pieces(2) + tail_pieces(0), False)
     pair_copy(1).start()
     scope("in3")
     super_wait(3)
     tail_cp[1].wait()
     super_start(5)
-    super_step(3)
-    tail_step(1)
+    in_block(super_pieces(3) + tail_pieces(1), False)
     pair_copy(2).start()
     chip_stage(1)
     scope("in4")
     super_wait(4)
-    super_step(4)
-    direct_stage(0)
+    w_cp[0].start()
+    in_block(super_pieces(4), False)
+    pair_copy(3).start()
     chip_stage(2)
     scope("in5")
     super_wait(5)
-    for cp in w_cp:
+    for cp in w_cp[1:]:
         cp.start()
-    super_step(5, 0, HALF)
+    in_block(super_pieces(5, 0, HALF), False)
+    direct_stage(0)
+    chip_stage(3)
+    in_block(super_pieces(5, HALF, SUPER), False)
     direct_stage(1)
-    super_step(5, HALF, SUPER)
-    direct_stage(2)
     back_stage(0)
 
     scope("forms")
@@ -316,6 +338,7 @@
     scope("wsq2")
     w_cp[nk].wait()
     w_sq.append(w_square_out())
+    back_stage(3)
 
     scope("wait1")
     for g in range(len(STAGED)):
@@ -349,7 +372,7 @@
         level = beta * (r_all / m_all) + mix * (scale * (scale * (sums[j] / n_all)) * (1.0 / m_all) + EPS_ONE)
         acol[pl.ds(ra, rn), :] = lax.rsqrt(r2 / level)
 
-    def u_square(ref, k, row0, m, cols, stat0, arow):
+    def u_square(ref, k, row0, m, cols, stat0, arow, unroll):
         rows = pl.ds(row0, m)
 
         def block(col, w, brow):
@@ -358,11 +381,11 @@
             return t * t
 
         def body(i, acc):
-            for q in range(4):
-                col = pl.multiple_of(i * 4 * LANES + q * LANES, LANES)
-                acc = acc + block(col, LANES, stat0 + i * 4 + q)
+            for q in range(unroll):
+                col = pl.multiple_of((i * unroll + q) * LANES, LANES)
+                acc = acc + block(col, LANES, stat0 + i * unroll + q)
             return acc
-        acc = lax.fori_loop(0, cols // LANES // 4, body, jnp.zeros((m, LANES), F32))
+        acc = lax.fori_loop(0, cols // LANES // unroll, body, jnp.zeros((m, LANES), F32))
         a = acol[pl.ds(arow, m), :]
         u = total(acc * a * a)
         rest = cols % LANES
@@ -372,8 +395,8 @@
         return u
 
     scope("upass")
-    u_sq = [u_square(di, k, 0, ni, nff, IN_ROW + IN_STEP * k, k * ni) for k in range(nk)]
-    u_sq.append(sum(u_square(do, None, row0, m, nd, OUT_ROW, nk * ni + row0)
+    u_sq = [u_square(di, k, 0, ni, nff, IN_ROW + IN_STEP * k, k * ni, 13) for k in range(nk)]
+    u_sq.append(sum(u_square(do, None, row0, m, nd, OUT_ROW, nk * ni + row0, 10)
                     for row0, m in ((0, 144), (144, 144), (288, no - 288))))
 
     scope("x2")
@@ -410,8 +433,8 @@
 B_IN = 32
 
 
-def update_kernel(di, do, wi, wo, rcol, acol, cnew, bden, kout, wi_out, ri_out, ci_out, wo_out, ro_out, co_out,
-                  buf_in, buf_out, sem_in, sem_out):
+def update_kernel(di, do, wi, wo, rcol, acol, cnew, bden, kout, wi_out, ri_hbm, ci_hbm, wo_out, ro_hbm, co_hbm,
+                  buf_in, buf_out, sem_in, sem_out, ri_out, ci_out, ro_out, co_out, sem_small):
     nk, ni, nff = di.shape
     no, nd = do.shape
     steps = ni // B_IN
@@ -425,6 +448,7 @@
     def step_of(w, g, b, a, kk):
         return w - kk * ((g * jnp.broadcast_to(b, g.shape)) * a)
 
+    scope("u_in")
     pend = [None] * buf_in.shape[0]
     for k in range(nk):
         kk = jnp.broadcast_to(kout[pl.ds(k, 1), :], (B_IN, LANES))
@@ -441,26 +465,7 @@
             cp = in_copy(k, i, slot)
             cp.start()
             pend[slot] = cp
-    pend_out = [None] * buf_out.shape[0]
-    for i in range(nd // CHUNK):
-        slot = i % buf_out.shape[0]
-        if pend_out[slot] is not None:
-            pend_out[slot].wait()
-        kk = jnp.broadcast_to(kout[pl.ds(nk, 1), :], (40, LANES))
-        bs = [bden[pl.ds(OUT_ROW + i * (CHUNK // LANES) + q, 1), :] for q in range(CHUNK // LANES)]
-
-        def rows_of(o, n, i=i, slot=slot, kk=kk, bs=bs):
-            r = pl.ds(o, n)
-            a = acol[pl.ds(nk * ni + o, n), :]
-            for q, b in enumerate(bs):
-                cc = pl.ds(i * CHUNK + q * LANES, LANES)
-                buf_out[slot, r, pl.ds(q * LANES, LANES)] = step_of(wo[r, cc], do[r, cc], b, a, kk[:n])
-
-        for o in range(0, no, 40):
-            rows_of(o, min(40, no - o))
-        cp = pltpu.make_async_copy(buf_out.at[slot], wo_out.at[:, pl.ds(i * CHUNK, CHUNK)], sem_out.at[slot])
-        cp.start()
-        pend_out[slot] = cp
+    scope("u_small")
     co_out[...] = cnew[pl.ds(OUT_ROW, nd // LANES), :]
     for k in range(nk):
         for c, n in widths(nff):
@@ -469,9 +474,36 @@
             ri_out[pl.ds(k, 1), pl.ds(c, n)] = column_to_lane(rcol[pl.ds(k * ni + c, n), :], n)
     for c, n in widths(no):
         ro_out[:, pl.ds(c, n)] = column_to_lane(rcol[pl.ds(nk * ni + c, -(-n // 8) * 8), :], n)
-    for cp in pend + pend_out:
+    small = [pltpu.make_async_copy(v, h, sem_small.at[i]) for i, (v, h) in enumerate(
+        ((ri_out, ri_hbm), (ci_out, ci_hbm), (ro_out, ro_hbm), (co_out, co_hbm)))]
+    for cp in small:
+        cp.start()
+    scope("u_out")
+    pend_out = [None] * buf_out.shape[0]
+    for i in range(nd // CHUNK):
+        slot = i % buf_out.shape[0]
+        if pend_out[slot] is not None:
+            pend_out[slot].wait()
+        kk = jnp.broadcast_to(kout[pl.ds(nk, 1), :], (40, LANES))
+        bs = [bden[pl.ds(OUT_ROW + i * (CHUNK // LANES) + q, 1), :] for q in range(CHUNK // LANES)]
+
+        def rows_of(o, n, i=i, slot=slot, kk=kk, bs=bs):
+            r = pl.ds(o, n)
+            a = acol[pl.ds(nk * ni + o, n), :]
+            for q, b in enumerate(bs):
+                cc = pl.ds(i * CHUNK + q * LANES, LANES)
+                buf_out[slot, r, pl.ds(q * LANES, LANES)] = step_of(wo[r, cc], do[r, cc], b, a, kk[:n])
+
+        for o in range(0, no, 40):
+            rows_of(o, min(40, no - o))
+        cp = pltpu.make_async_copy(buf_out.at[slot], wo_out.at[:, pl.ds(i * CHUNK, CHUNK)], sem_out.at[slot])
+        cp.start()
+        pend_out[slot] = cp
+    scope("u_wait")
+    for cp in pend + pend_out + small:
         if cp is not None:
             cp.wait()
+    scope(None)
 
 
 def solution(mesh):
@@ -504,7 +536,7 @@
             out_specs=[vm] * len(a_out),
             scratch_shapes=[
                 pltpu.VMEM((ni, t), BF16), pltpu.VMEM((no, t), BF16), pltpu.VMEM((t, nd), BF16),
-                pltpu.VMEM((SLOTS, SUPER, t), BF16), pltpu.VMEM((nk, tail_cols, t), BF16),
+                pltpu.VMEM((SLOTS, SUPER, t), BF16), pltpu.VMEM((nk, tail_cols, t), BF16), pltpu.VMEM((2, 256, ni), F32),
                 pltpu.VMEM((nk, ni), F32), pltpu.VMEM((nk, nff), F32), pltpu.VMEM((1, no), F32),
                 pltpu.VMEM((nd // LANES, LANES), F32),
                 stat, stat, stat, pltpu.VMEM((n_dev // 2, STAT_ROWS, LANES), F32),
@@ -527,8 +559,11 @@
             update_kernel,
             out_shape=b_out,
             in_specs=[vm] * len(outs),
-            out_specs=[hb, vm, vm, hb, vm, vm],
-            scratch_shapes=[pltpu.VMEM((4, B_IN, nff), F32), pltpu.VMEM((2, no, CHUNK), F32), dma((4,)), dma((2,))],
+            out_specs=[hb] * 6,
+            scratch_shapes=[pltpu.VMEM((nk * ni // B_IN, B_IN, nff), F32), pltpu.VMEM((nd // CHUNK, no, CHUNK), F32),
+                            dma((nk * ni // B_IN,)), dma((nd // CHUNK,)),
+                            pltpu.VMEM((nk, ni), F32), pltpu.VMEM((nk, nff), F32), pltpu.VMEM((1, no), F32),
+                            pltpu.VMEM((nd // LANES, LANES), F32), dma((4,))],
             compiler_params=pltpu.CompilerParams(vmem_limit_bytes=SCOPED),
             name="update",
         )(*outs)

time: 38.2 us -> 36 us (0.942)
  Pallas kernels: 34.6 us -> 32.4 us
    pallas_call x1, Pallas kernels: 6.3 us -> 5.03 us  [local_step(): pl.pallas_call(update_kernel, out_shape=b_out, in_specs=[vm] * len(outs),...]
    pallas_call x1, Pallas kernels: 28.3 us -> 27.4 us  [local_step(): pl.pallas_call(lambda *refs: stats_kernel(n_dev, *refs), out_shape=a_out,...]
where the time goes in v3:
time: 36 us; the launch traced here: 35.8 us
  Pallas kernels  32.4 us (90%)
  between operations  3.39 us (9%)
    pallas_call x1, Pallas kernels, local_step(): pl.pallas_call(lambda *refs: stats_kernel(n_dev, *refs), out_shape=a_out,...  27.4 us
    pallas_call x1, Pallas kernels, local_step(): pl.pallas_call(update_kernel, out_shape=b_out, in_specs=[vm] * len(outs),...  5.03 us

profile of v3, /device:TPU:0, one launch (start us, length us, event | category | flops | bytes accessed | tf_op | source)
XLA Modules:
  0.0 35.8 jit_solution(15269478439968094575)
XLA Ops:
  3.2 27.4 %stats.1 = (f32[2,160,6720]{2,1,0:T(8,128)S(1)}, f32[420,2560]{1,0:T(8,128)S(1)}, f32[2,160,6720]{2,1,0:T(8,128)S(1)}, f32[420,2560]{1,0:T(8,128)S(1)}, f32[744,...) custom-call(bf16[160,1024]{1,0:T(8,128)(2,1)} %bitcast.9, ...), custom_call_target="tpu_custom_call" | custom-call | tf_op jit(solution)/shard_map/stats/pallas_call | solution.py:532
  30.6 5.0 %update.1 = (f32[2,160,6720]{2,1,0:T(8,128)}, f32[2,160]{1,0:T(2,128)}, f32[2,6720]{1,0:T(2,128)}, f32[420,2560]{1,0:T(8,128)}, f32[1,420]{1,0:T(1,128)}, /*index=5*/f32[20,128]{1,0:T(8,128)}) custom-call(f32[2,160,6720]{2,1,0:T(8,128)S(1)} %get-tuple-element.21.di, f32[420,2560]{1,0:T(8,128)S(1)} %get-tuple-element.22.do, ...), custom_call_target="tpu_custom_call" | custom-call | tf_op jit(solution)/shard_map/update/pallas_call | solution.py:558

commit v4 on v3

--- a/solution.py
+++ b/solution.py
@@ -54,7 +54,7 @@
 def stats_kernel(n_dev, x_hbm, h_hbm, dyo_hbm, dyi_hbm, wi_hbm, wo_hbm, ri_hbm, ci_hbm, ro_hbm, co_hbm,
                  beta_s, rel_s, crms_s, cnorm_s,
                  di, do, wi, wo, rcol, acol, cnew, bden, kout,
-                 x_v, h_v, dyo_v, ring, tail, raw, ri_v, ci_v, ro_v, co_v, part, pair, tot, recv, recv_all, cden, rsum, recv2,
+                 x_v, h_v, dyo_v, ring, tail, raw, turned, ri_v, ci_v, ro_v, co_v, part, pair, tot, recv, recv_all, cden, rsum, recv2,
                  in_sem, dyo_sem, ring_sem, tail_sem, w_sem, pair_sem, chip_sem, back_sem, all_sem, two_sem):
     me = lax.axis_index('tp')
     core = lax.rem(me, 2)
@@ -96,10 +96,11 @@
         ((ro_hbm, ro_v), (ri_hbm, ri_v), (co_hbm, co_v), (ci_hbm, ci_v), (h_hbm, h_v), (x_hbm, x_v)))]
     dyo_cp = [pltpu.make_async_copy(dyo_hbm.at[:, pl.ds(c, CHUNK)], dyo_v.at[:, pl.ds(c, CHUNK)],
                                     dyo_sem.at[c // CHUNK]) for c in range(0, nd, CHUNK)]
-    for cp in small[4:5] + dyo_cp[:2]:
+    for cp in small[4:5] + dyo_cp[:1]:
         cp.start()
     part[...] = jnp.zeros_like(part)
     rsum[...] = jnp.zeros_like(rsum)
+    dyo_cp[1].start()
 
     def halves(start, size, c):
         return pl.ds(pl.multiple_of(start + c * (size // 2), 8), size // 2)
@@ -177,9 +178,9 @@
             f()
         deferred.clear()
 
-    def finish_in(k, col, g):
-        g = g.T
-        di[k, :, pl.ds(col, g.shape[1])] = g
+    def finish_in(k, col, g, store):
+        if store:
+            di[k, :, pl.ds(col, g.shape[1])] = g
         square_sums(g, k * ni, IN_ROW + IN_STEP * k + col // LANES)
 
     def finish_out(col):
@@ -187,13 +188,24 @@
 
     def in_block(pieces, defer):
         for j, (k, col, n, ref) in enumerate(pieces):
-            g = lax.dot_general(ref[...], x_v[...], (((1,), (1,)), ((), ())), preferred_element_type=F32)
             slot = j - len(pieces) + 2
-            if defer and slot >= 0:
-                raw[slot, pl.ds(0, n), :] = g
-                deferred.append(lambda k=k, col=col, n=n, slot=slot: finish_in(k, col, raw[slot, pl.ds(0, n), :]))
+            defer_this = defer and slot >= 0
+            if j%2==1:
+                turned[j % 4, :, pl.ds(0, n)] = ref[...].T
+                g = jnp.dot(x_v[...], turned[j % 4, :, pl.ds(0, n)], preferred_element_type=F32)
+                if defer_this:
+                    di[k, :, pl.ds(col, n)] = g
+                    deferred.append(lambda k=k, col=col, n=n: finish_in(k, col, di[k, :, pl.ds(col, n)], False))
+                else:
+                    finish_in(k, col, g, True)
             else:
-                finish_in(k, col, g)
+                g = lax.dot_general(ref[...], x_v[...], (((1,), (1,)), ((), ())), preferred_element_type=F32)
+                if defer_this:
+                    raw[slot, pl.ds(0, n), :] = g
+                    deferred.append(lambda k=k, col=col, n=n, slot=slot:
+                                    finish_in(k, col, raw[slot, pl.ds(0, n), :].T, True))
+                else:
+                    finish_in(k, col, g.T, True)
 
     def super_pieces(i, start=0, stop=SUPER):
         k, c = sequence[i]
@@ -245,7 +257,7 @@
     super_start(2)
     tail_cp[0].start()
     flush()
-    in_block(super_pieces(0), True)
+    in_block(super_pieces(0), False)
     pl.semaphore_wait(barrier, n_dev - 1)
     pair_copy(0).start()
     scope("in1")
@@ -253,7 +265,7 @@
     super_start(3)
     tail_cp[1].start()
     flush()
-    in_block(super_pieces(1), True)
+    in_block(super_pieces(1), False)
     chip_stage(0)
     scope("in2")
     super_wait(2)
@@ -372,7 +384,7 @@
         level = beta * (r_all / m_all) + mix * (scale * (scale * (sums[j] / n_all)) * (1.0 / m_all) + EPS_ONE)
         acol[pl.ds(ra, rn), :] = lax.rsqrt(r2 / level)
 
-    def u_square(ref, k, row0, m, cols, stat0, arow, unroll):
+    def u_square(ref, k, row0, m, cols, stat0, arow):
         rows = pl.ds(row0, m)
 
         def block(col, w, brow):
@@ -380,29 +392,27 @@
             t = ref[idx] * jnp.broadcast_to(bden[pl.ds(brow, 1), pl.ds(0, w)], (m, w))
             return t * t
 
-        def body(i, acc):
-            for q in range(unroll):
-                col = pl.multiple_of((i * unroll + q) * LANES, LANES)
-                acc = acc + block(col, LANES, stat0 + i * unroll + q)
-            return acc
-        acc = lax.fori_loop(0, cols // LANES // unroll, body, jnp.zeros((m, LANES), F32))
+        acc = jnp.zeros((m, LANES), F32)
+        for q in range(cols // LANES):
+            acc = acc + block(q * LANES, LANES, stat0 + q)
         a = acol[pl.ds(arow, m), :]
-        u = total(acc * a * a)
+        u = jnp.sum(acc * a * a, axis=0, keepdims=True)
         rest = cols % LANES
         if rest:
             a = acol[pl.ds(arow, m), pl.ds(0, rest)]
-            u = u + total(block(cols - rest, rest, stat0 + cols // LANES) * a * a)
+            r = jnp.sum(block(cols - rest, rest, stat0 + cols // LANES) * a * a, axis=0, keepdims=True)
+            u = u + jnp.concatenate([r, jnp.zeros((1, LANES - rest), F32)], axis=1)
         return u
 
     scope("upass")
-    u_sq = [u_square(di, k, 0, ni, nff, IN_ROW + IN_STEP * k, k * ni, 13) for k in range(nk)]
-    u_sq.append(sum(u_square(do, None, row0, m, nd, OUT_ROW, nk * ni + row0, 10)
+    u_sq = [u_square(di, k, 0, ni, nff, IN_ROW + IN_STEP * k, k * ni) for k in range(nk)]
+    u_sq.append(sum(u_square(do, None, row0, m, nd, OUT_ROW, nk * ni + row0)
                     for row0, m in ((0, 144), (144, 144), (288, no - 288))))
 
     scope("x2")
     msg = jnp.zeros((1, LANES), F32)
     for j in range(3):
-        msg = msg + jnp.where(lane == j, u_sq[j], 0.0) + jnp.where(lane == 3 + j, w_sq[j], 0.0)
+        msg = msg + jnp.where(lane == j, jnp.sum(u_sq[j], axis=1, keepdims=True), 0.0) + jnp.where(lane == 3 + j, w_sq[j], 0.0)
     recv2[me] = msg
     for d in range(1, n_dev):
         two_copy(d).start()
@@ -536,7 +546,7 @@
             out_specs=[vm] * len(a_out),
             scratch_shapes=[
                 pltpu.VMEM((ni, t), BF16), pltpu.VMEM((no, t), BF16), pltpu.VMEM((t, nd), BF16),
-                pltpu.VMEM((SLOTS, SUPER, t), BF16), pltpu.VMEM((nk, tail_cols, t), BF16), pltpu.VMEM((2, 256, ni), F32),
+                pltpu.VMEM((SLOTS, SUPER, t), BF16), pltpu.VMEM((nk, tail_cols, t), BF16), pltpu.VMEM((2, 256, ni), F32), pltpu.VMEM((4, t, 256), BF16),
                 pltpu.VMEM((nk, ni), F32), pltpu.VMEM((nk, nff), F32), pltpu.VMEM((1, no), F32),
                 pltpu.VMEM((nd // LANES, LANES), F32),
                 stat, stat, stat, pltpu.VMEM((n_dev // 2, STAT_ROWS, LANES), F32),

time: 36 us -> 34.8 us (0.967)
  Pallas kernels: 32.4 us -> 31.2 us
    pallas_call x1, Pallas kernels: 27.4 us -> 26.2 us  [local_step(): pl.pallas_call(lambda *refs: stats_kernel(n_dev, *refs), out_shape=a_out,...]
where the time goes in v4:
time: 34.8 us; the launch traced here: 34.6 us
  Pallas kernels  31.2 us (90%)
  between operations  3.39 us (10%)
    pallas_call x1, Pallas kernels, local_step(): pl.pallas_call(lambda *refs: stats_kernel(n_dev, *refs), out_shape=a_out,...  26.2 us
    pallas_call x1, Pallas kernels, local_step(): pl.pallas_call(update_kernel, out_shape=b_out, in_specs=[vm] * len(outs),...  5.03 us

profile of v4, /device:TPU:0, one launch (start us, length us, event | category | flops | bytes accessed | tf_op | source)
XLA Modules:
  0.0 34.6 jit_solution(13262613508029837100)
XLA Ops:
  3.2 26.2 %stats.1 = (f32[2,160,6720]{2,1,0:T(8,128)S(1)}, f32[420,2560]{1,0:T(8,128)S(1)}, f32[2,160,6720]{2,1,0:T(8,128)S(1)}, f32[420,2560]{1,0:T(8,128)S(1)}, f32[744,...) custom-call(bf16[160,1024]{1,0:T(8,128)(2,1)} %bitcast.9, ...), custom_call_target="tpu_custom_call" | custom-call | tf_op jit(solution)/shard_map/stats/pallas_call | solution.py:542
  29.4 5.0 %update.1 = (f32[2,160,6720]{2,1,0:T(8,128)}, f32[2,160]{1,0:T(2,128)}, f32[2,6720]{1,0:T(2,128)}, f32[420,2560]{1,0:T(8,128)}, f32[1,420]{1,0:T(1,128)}, /*index=5*/f32[20,128]{1,0:T(8,128)}) custom-call(f32[2,160,6720]{2,1,0:T(8,128)S(1)} %get-tuple-element.21.di, f32[420,2560]{1,0:T(8,128)S(1)} %get-tuple-element.22.do, ...), custom_call_target="tpu_custom_call" | custom-call | tf_op jit(solution)/shard_map/update/pallas_call | solution.py:568

commit v5 on v4

--- a/solution.py
+++ b/solution.py
@@ -15,6 +15,7 @@
 OUT_ROW, IN_ROW, IN_STEP, STAT_ROWS = 0, 32, 64, 160
 SCALAR_ROW = 24
 STAGED = ((0, 32), (32, 64), (128, 32), (112, 16))
+WIDE = 3
 DIRECT_ROW = 96
 DIRECT = ((96, 8), (104, 8))
 CHUNK = 512
@@ -131,6 +132,18 @@
 
     def bytes_of(ref, sem):
         pltpu.make_async_copy(ref, ref, sem).wait()
+
+    def wide_stage(g):
+        rows = halves(*STAGED[g], core)
+        pair_copy(g).wait_recv()
+        recv[chip, rows, :] = part[rows, :] + pair[rows, :]
+        for d in range(1, n_dev):
+            ref = recv.at[chip, rows, :]
+            remote(ref, ref, chip_sem.at[g], lax.rem(me + d, n_dev)).start()
+
+    def wide_bytes(g, i):
+        n = STAGED[g][1] // 2 * (n_dev - 1)
+        bytes_of(recv.at[pl.ds(0, 5), pl.ds(0, n // 5), :], chip_sem.at[g, i])
 
     def chip_stage(g):
         rows = halves(*STAGED[g], core)
@@ -230,14 +243,13 @@
         cp.start()
     out_piece(0, CHUNK)
     dyo_cp[1].wait()
-    for cp in dyo_cp[4:] + small[5:6] + small[:4]:
+    for cp in small[:4] + dyo_cp[4:] + small[5:6]:
         cp.start()
-    half_copy(0, 0).start()
+    super_start(0)
     scope("out1")
     dyo_cp[2].wait()
     flush()
     out_piece(CHUNK, 3 * CHUNK)
-    half_copy(0, 1).start()
     super_start(1)
     scope("out2")
     for cp in dyo_cp[3:]:
@@ -293,7 +305,7 @@
         cp.start()
     in_block(super_pieces(5, 0, HALF), False)
     direct_stage(0)
-    chip_stage(3)
+    wide_stage(3)
     in_block(super_pieces(5, HALF, SUPER), False)
     direct_stage(1)
     back_stage(0)
@@ -350,12 +362,17 @@
     scope("wsq2")
     w_cp[nk].wait()
     w_sq.append(w_square_out())
-    back_stage(3)
 
     scope("wait1")
-    for g in range(len(STAGED)):
+    for g in range(WIDE):
         ref = tot.at[halves(*STAGED[g], 1 - core), :]
         bytes_of(ref, back_sem.at[g, 1])
+    wide_bytes(WIDE, 1)
+    rows = pl.ds(*STAGED[WIDE])
+    t = recv[0, rows, :]
+    for c in range(1, n_chip):
+        t = t + recv[c, rows, :]
+    tot[rows, :] = t
     for g in range(len(DIRECT)):
         start, size = DIRECT[g]
         rows = pl.ds(start - DIRECT_ROW, size)
@@ -416,7 +433,9 @@
     recv2[me] = msg
     for d in range(1, n_dev):
         two_copy(d).start()
-    for g in range(len(STAGED)):
+    pair_copy(WIDE).wait_send()
+    wide_bytes(WIDE, 0)
+    for g in range(WIDE):
         pair_copy(g).wait_send()
         back_copy(g).wait_send()
         bytes_of(recv.at[pl.ds(0, n_chip - 1), halves(*STAGED[g], core), :], chip_sem.at[g, 0])

time: 34.8 us -> 34.4 us (0.989)
  no operation moved by 1% of the time
where the time goes in v5:
time: 34.4 us; the launch traced here: 34.3 us
  Pallas kernels  30.9 us (90%)
  between operations  3.39 us (10%)
    pallas_call x1, Pallas kernels, local_step(): pl.pallas_call(lambda *refs: stats_kernel(n_dev, *refs), out_shape=a_out,...  25.9 us
    pallas_call x1, Pallas kernels, local_step(): pl.pallas_call(update_kernel, out_shape=b_out, in_specs=[vm] * len(outs),...  5.03 us

profile of v5, /device:TPU:0, one launch (start us, length us, event | category | flops | bytes accessed | tf_op | source)
XLA Modules:
  0.0 34.3 jit_solution(14218650555416283869)
XLA Ops:
  3.2 25.9 %stats.1 = (f32[2,160,6720]{2,1,0:T(8,128)S(1)}, f32[420,2560]{1,0:T(8,128)S(1)}, f32[2,160,6720]{2,1,0:T(8,128)S(1)}, f32[420,2560]{1,0:T(8,128)S(1)}, f32[744,...) custom-call(bf16[160,1024]{1,0:T(8,128)(2,1)} %bitcast.9, ...), custom_call_target="tpu_custom_call" | custom-call | tf_op jit(solution)/shard_map/stats/pallas_call | solution.py:561
  29.1 5.0 %update.1 = (f32[2,160,6720]{2,1,0:T(8,128)}, f32[2,160]{1,0:T(2,128)}, f32[2,6720]{1,0:T(2,128)}, f32[420,2560]{1,0:T(8,128)}, f32[1,420]{1,0:T(1,128)}, /*index=5*/f32[20,128]{1,0:T(8,128)}) custom-call(f32[2,160,6720]{2,1,0:T(8,128)S(1)} %get-tuple-element.21.di, f32[420,2560]{1,0:T(8,128)S(1)} %get-tuple-element.22.do, ...), custom_call_target="tpu_custom_call" | custom-call | tf_op jit(solution)/shard_map/update/pallas_call | solution.py:587

commit v6 on v5

--- a/solution.py
+++ b/solution.py
@@ -101,7 +101,8 @@
         cp.start()
     part[...] = jnp.zeros_like(part)
     rsum[...] = jnp.zeros_like(rsum)
-    dyo_cp[1].start()
+    for cp in dyo_cp[1:3]:
+        cp.start()
 
     def halves(start, size, c):
         return pl.ds(pl.multiple_of(start + c * (size // 2), 8), size // 2)
@@ -239,13 +240,14 @@
     scope("out")
     small[4].wait()
     dyo_cp[0].wait()
-    for cp in dyo_cp[2:4]:
+    for cp in dyo_cp[3:] + small[5:6]:
         cp.start()
+    half_copy(0, 0).start()
     out_piece(0, CHUNK)
     dyo_cp[1].wait()
-    for cp in small[:4] + dyo_cp[4:] + small[5:6]:
+    for cp in small[:4]:
         cp.start()
-    super_start(0)
+    half_copy(0, 1).start()
     scope("out1")
     dyo_cp[2].wait()
     flush()

time: 34.4 us -> 34.3 us (level)
  no operation moved by 1% of the time
where the time goes in v6:
time: 34.3 us; the launch traced here: 34.2 us
  Pallas kernels  30.8 us (90%)
  between operations  3.39 us (10%)
    pallas_call x1, Pallas kernels, local_step(): pl.pallas_call(lambda *refs: stats_kernel(n_dev, *refs), out_shape=a_out,...  25.8 us
    pallas_call x1, Pallas kernels, local_step(): pl.pallas_call(update_kernel, out_shape=b_out, in_specs=[vm] * len(outs),...  5.03 us

profile of v6, /device:TPU:0, one launch (start us, length us, event | category | flops | bytes accessed | tf_op | source)
XLA Modules:
  0.0 34.2 jit_solution(12208255839209453916)
XLA Ops:
  3.2 25.8 %stats.1 = (f32[2,160,6720]{2,1,0:T(8,128)S(1)}, f32[420,2560]{1,0:T(8,128)S(1)}, f32[2,160,6720]{2,1,0:T(8,128)S(1)}, f32[420,2560]{1,0:T(8,128)S(1)}, f32[744,...) custom-call(bf16[160,1024]{1,0:T(8,128)(2,1)} %bitcast.9, ...), custom_call_target="tpu_custom_call" | custom-call | tf_op jit(solution)/shard_map/stats/pallas_call | solution.py:563
  29.0 5.0 %update.1 = (f32[2,160,6720]{2,1,0:T(8,128)}, f32[2,160]{1,0:T(2,128)}, f32[2,6720]{1,0:T(2,128)}, f32[420,2560]{1,0:T(8,128)}, f32[1,420]{1,0:T(1,128)}, /*index=5*/f32[20,128]{1,0:T(8,128)}) custom-call(f32[2,160,6720]{2,1,0:T(8,128)S(1)} %get-tuple-element.21.di, f32[420,2560]{1,0:T(8,128)S(1)} %get-tuple-element.22.do, ...), custom_call_target="tpu_custom_call" | custom-call | tf_op jit(solution)/shard_map/update/pallas_call | solution.py:589
